TPU v7x, 32 devices: a whole 2x2x4 slice. The times are simulated.
32 devices in a mesh: dp: 4 (over z), tp: 8 (over y, x, core).
Axes of the slice: x: 2, y: 2, z: 4, core: 2. Of those that a mesh axis runs over, the one named last changes fastest.
Arguments:
- tokens: bfloat16 [12, 768, 5120], P('dp'), parts along dimension 0
- positions: int32 [12, 768], P('dp'), parts along dimension 0
- lengths: int32 [12], P('dp'), parts along dimension 0
- norm_attn: bfloat16 [5120], replicated
- norm_mlp: bfloat16 [5120], replicated
- q_gain: bfloat16 [128], replicated
- k_gain: bfloat16 [128], replicated
- w_query: bfloat16 [5120, 5120], P(None, 'tp')
- w_key: bfloat16 [5120, 1024], replicated
- w_value: bfloat16 [5120, 1024], replicated
- w_out: bfloat16 [5120, 5120], P('tp')
- w_gate: bfloat16 [5120, 17408], P(None, 'tp')
- w_up: bfloat16 [5120, 17408], P(None, 'tp')
- w_down: bfloat16 [17408, 5120], P('tp')
Outputs:
- output 1: bfloat16 [12, 768, 5120], P('dp'), parts along dimension 0
- output 2: bfloat16 [12, 768, 8, 128], P('dp', None, 'tp'), parts along dimension 0
- output 3: bfloat16 [12, 768, 8, 128], P('dp', None, 'tp'), parts along dimension 0
There are 4 independent parts. A program takes and returns all parts, laid end to end along the dimension named above; an argument that names none is the same for every part.
All inputs are finite; a program needn't handle non-finite values.
Results may differ from a plain program's by a relative error of at most 0.0142364.
Values are sent between devices in bfloat16 or wider.
A program may use at most 1 GiB of HBM per device.

v0:
```python
import functools
import jax
import jax.numpy as jnp
from jax import lax
from jax.sharding import PartitionSpec as P

EPSILON = 1e-6
ROPE_THETA = 1000000.0


def rms_scale(values, gain_vec):
    mean_sq = jnp.mean(values * values, axis=-1, keepdims=True)
    return values * lax.rsqrt(mean_sq + EPSILON) * gain_vec.astype(jnp.float32)


def rope_tables(positions, half_dim):
    inv_freq = ROPE_THETA ** (-jnp.arange(half_dim, dtype=jnp.float32) / half_dim)
    angles = positions.astype(jnp.float32)[:, :, None] * inv_freq
    return jnp.cos(angles)[:, :, None, :], jnp.sin(angles)[:, :, None, :]


def rope_apply(values, cosine, sine_tab):
    half_dim = values.shape[-1] // 2
    first_half = values[..., :half_dim]
    second_half = values[..., half_dim:]
    return jnp.concatenate([first_half * cosine - second_half * sine_tab, second_half * cosine + first_half * sine_tab], axis=-1)


def local_attention(q_rot, k_rot, v_vals, lengths):
    seq_len, head_dim = k_rot.shape[1], k_rot.shape[2]
    scores = jnp.einsum('bshd,btd->bhst', q_rot, k_rot, preferred_element_type=jnp.float32) * head_dim ** -0.5
    row_idx = jnp.arange(seq_len)[:, None]
    col_idx = jnp.arange(seq_len)[None, :]
    allowed = (col_idx <= row_idx)[None, None] & (col_idx[None, None] < lengths[:, None, None, None])
    attn_probs = jax.nn.softmax(jnp.where(allowed, scores, -1e30), axis=-1).astype(jnp.bfloat16)
    return jnp.einsum('bhst,btd->bshd', attn_probs, v_vals, preferred_element_type=jnp.float32).astype(jnp.bfloat16)


def layer_body(tokens, positions, lengths, norm_attn, norm_mlp, q_gain, k_gain, w_query, w_key, w_value, w_out, w_gate, w_up, w_down, tp_size):
    num_prompts, seq_len, hidden_dim = tokens.shape
    head_dim = q_gain.shape[0]
    local_heads = w_query.shape[1] // head_dim
    kv_heads = w_key.shape[1] // head_dim
    kv_index = lax.axis_index('tp') // (tp_size // kv_heads)
    rows_n = num_prompts * seq_len
    tokens_f32 = tokens.reshape(rows_n, hidden_dim).astype(jnp.float32)
    normed = rms_scale(tokens_f32, norm_attn).astype(jnp.bfloat16)
    w_key_head = lax.dynamic_slice_in_dim(w_key, kv_index * head_dim, head_dim, axis=1)
    w_value_head = lax.dynamic_slice_in_dim(w_value, kv_index * head_dim, head_dim, axis=1)
    q_proj = jnp.dot(normed, w_query, preferred_element_type=jnp.float32).reshape(num_prompts, seq_len, local_heads, head_dim)
    k_proj = jnp.dot(normed, w_key_head, preferred_element_type=jnp.float32).reshape(num_prompts, seq_len, 1, head_dim)
    v_vals = jnp.dot(normed, w_value_head, preferred_element_type=jnp.float32).astype(jnp.bfloat16).reshape(num_prompts, seq_len, head_dim)
    cosine, sine_tab = rope_tables(positions, head_dim // 2)
    q_rot = rope_apply(rms_scale(q_proj, q_gain), cosine, sine_tab).astype(jnp.bfloat16)
    k_rot = rope_apply(rms_scale(k_proj, k_gain), cosine, sine_tab).astype(jnp.bfloat16).reshape(num_prompts, seq_len, head_dim)
    valid_mask = (jnp.arange(seq_len)[None, :] < lengths[:, None])[:, :, None]
    k_cache = jnp.where(valid_mask, k_rot, 0).astype(jnp.bfloat16)[:, :, None, :]
    v_cache = jnp.where(valid_mask, v_vals, 0).astype(jnp.bfloat16)[:, :, None, :]
    attn_rows = local_attention(q_rot, k_rot, v_vals, lengths).reshape(rows_n, local_heads * head_dim)
    attn_part = jnp.dot(attn_rows, w_out, preferred_element_type=jnp.float32).astype(jnp.bfloat16)
    attn_sum = lax.psum(attn_part, 'tp')
    hidden = (tokens_f32 + attn_sum.astype(jnp.float32)).astype(jnp.bfloat16).astype(jnp.float32)
    normed_mlp = rms_scale(hidden, norm_mlp).astype(jnp.bfloat16)
    gate_proj = jnp.dot(normed_mlp, w_gate, preferred_element_type=jnp.float32)
    up_proj = jnp.dot(normed_mlp, w_up, preferred_element_type=jnp.float32)
    gated = (jax.nn.silu(gate_proj) * up_proj).astype(jnp.bfloat16)
    mlp_part = jnp.dot(gated, w_down, preferred_element_type=jnp.float32).astype(jnp.bfloat16)
    mlp_sum = lax.psum(mlp_part, 'tp')
    output = (hidden + mlp_sum.astype(jnp.float32)).astype(jnp.bfloat16).reshape(num_prompts, seq_len, hidden_dim)
    return output, k_cache, v_cache


def solution(mesh):
    body = functools.partial(layer_body, tp_size=mesh.shape['tp'])
    in_specs = (P('dp', None, None), P('dp', None), P('dp'), P(), P(), P(), P(), P(None, 'tp'), P(), P(), P('tp', None), P(None, 'tp'), P(None, 'tp'), P('tp', None))
    out_specs = (P('dp', None, None), P('dp', None, 'tp', None), P('dp', None, 'tp', None))
    return jax.shard_map(body, mesh=mesh, in_specs=in_specs, out_specs=out_specs, check_vma=False)
```

profile of v0, /device:TPU:0, one launch (start us, length us, event | category | flops | bytes accessed | tf_op | source)
XLA Modules:
  0.0 1015.6 jit_solution(9244259470562840757)
XLA Ops:
  10.2 9.9 fusion.5
  20.2 9.5 copy.23
  29.7 22.6 %multiply_reduce_fusion = (f32[3,768,5]{1,2,0:T(8,128)S(1)}, f32[3,768,5,128]{1,3,2,0:T(8,128)}) fusion(bf16[5,128,5120,1]{2,1,0,3:T(8,128)(2,1)} %bitcast.80, bf16[3,768,5120]{2,1,0:T(8,128)(2,1)} %param.14, f32[5120]{0:T(1024)S(1)} %convert_element_type.88, f32[3,768]{1,0:T(4,128)S(1)} %add_rsqrt_fusion.3), kind=kOutput, calls=%fused_computation.35 | convolution fusion | flops 15149618176 | bytes 36120576 | tf_op jit(solution)/shard_map/dot_general | solution.py:50
  52.3 21.8 %fusion.9 = bf16[2304,5120]{1,0:T(8,128)(2,1)} fusion(bf16[3,768,5120]{2,1,0:T(8,128)(2,1)} %param.14, f32[5120]{0:T(1024)S(1)} %convert_element_type.88, f32[2304]{0:T(1024)S(1)} %rsqrt.40), kind=kLoop, calls=%fused_computation.16 | loop fusion | flops 47185920 | bytes 47215616 | tf_op jit(solution)/shard_map/convert_element_type | solution.py:47
  74.1 14.6 %convolution_convert_fusion.2 = bf16[2304,128]{1,0:T(8,128)(2,1)} fusion(bf16[2304,5120]{1,0:T(8,128)(2,1)} %fusion.9, bf16[5120,1024]{1,0:T(8,128)(2,1)} %param.23, s32[]{:T(128)S(6)} %select_n.32), kind=kOutput, calls=%fused_computation.36 | convolution fusion | flops 3020193792 | bytes 25493508 | tf_op jit(solution)/shard_map/dot_general | solution.py:52
  89.1 7.8 multiply_reduce_fusion.1
  96.9 2.1 multiply_cosine_fusion.1
  99.4 5.3 fusion.34
  104.7 1.9 broadcast_and_fusion
  106.6 3.7 multiply_multiply_fusion
  110.3 2.6 subtract_convert_fusion
  112.9 18.9 %fusion.47 = (f32[3,5,768]{2,1,0:T(8,128)}, f32[3,5,768,768]{2,3,1,0:T(8,128)}) fusion(pred[3,768,768]{1,2,0:T(8,128)(4,1)S(1)} %copy-done.5, bf16[3,768,5,64]{1,3,2,0:T(8,128)(2,1)} %get-tuple-element.12, bf16[3,768,5,64]{1,3,2,0:T(8,128)(2,1)} %get-tuple-element.11, bf16[3,768,64]{2,1,0:T(8,128)(2,1)S(1)} %bitcast.83, bf16[3,768,64]{2,1,0:T(8,128)(2,1)S(1)} %bitcast.82), kind=kOutput, calls=%fused_computation.77 | convolution fusion | flops 2307392256 | bytes 40743936 | tf_op jit(solution)/shard_map/sub | solution.py:35
  131.8 12.8 %convert_bitcast_fusion = bf16[3,768,5,128]{1,3,2,0:T(8,128)(2,1)S(1)} fusion(bf16[3,768,128,1]{2,1,3,0:T(8,128)(2,1)S(1)} %bitcast.85, f32[3,5,768,768]{2,3,1,0:T(8,128)} %get-tuple-element.24, f32[3,5,768]{2,1,0:T(8,128)} %get-tuple-element.23), kind=kOutput, calls=%fused_computation.39 | convolution fusion | flops 2284093440 | bytes 38974464 | tf_op jit(solution)/shard_map/bhst,btd->bshd/dot_general | solution.py:36
  144.6 2.5 copy.27
  147.7 25.4 %convolution_convert_fusion.1 = bf16[2304,5120]{1,0:T(8,128)(2,1)} fusion(bf16[2304,640]{0,1:T(8,128)(2,1)S(1)} %bitcast.81, bf16[640,5120]{1,0:T(8,128)(2,1)} %param.24), kind=kOutput, calls=%fused_computation.22 | convolution fusion | flops 15111290880 | bytes 33095680 | tf_op jit(solution)/shard_map/dot_general | solution.py:60
  173.9 292.0 %all-reduce.3.cloned.1.call-done = bf16[2304,5120]{1,0:T(8,128)(2,1)} async-done(((bf16[2304,5120]{1,0:T(8,128)(2,1)}), bf16[2304,5120]{1,0:T(8,128)(2,1)}) %all-reduce.3.cloned.1.call-update) | async-done | bytes 23592976 | tf_op jit(solution)/shard_map/psum | solution.py:61
  465.9 28.1 %fusion.1 = (f32[2304]{0:T(1024)S(1)}, bf16[2304,5120]{1,0:T(8,128)(2,1)}) fusion(bf16[2304,5120]{1,0:T(8,128)(2,1)} %all-reduce.3.cloned.1.call-done, bf16[3,768,5120]{2,1,0:T(8,128)(2,1)} %param.14), kind=kLoop, calls=%fused_computation.4 | loop fusion | flops 82573056 | bytes 70788096 | tf_op jit(solution)/shard_map/reduce_sum | solution.py:12
  493.9 66.4 %fusion.23 = f32[2304,2176]{1,0:T(8,128)} fusion(bf16[5120,2176]{1,0:T(8,128)(2,1)} %param.25, bf16[2304,5120]{1,0:T(8,128)(2,1)} %get-tuple-element.10, f32[5120]{0:T(1024)S(1)} %convert_element_type.102, f32[2304]{0:T(1024)S(1)} %add_rsqrt_fusion.1), kind=kOutput, calls=%fused_computation.33 | convolution fusion | flops 51385466880 | bytes 65958912 | tf_op jit(solution)/shard_map/dot_general | solution.py:64
  560.3 67.6 %fusion.19 = bf16[2304,2176]{1,0:T(8,128)(2,1)} fusion(bf16[5120,2176]{1,0:T(8,128)(2,1)} %param.26, f32[2304,2176]{1,0:T(8,128)} %fusion.23, bf16[2304,5120]{1,0:T(8,128)(2,1)} %get-tuple-element.10, f32[5120]{0:T(1024)S(1)} %convert_element_type.102, f32[2304]{0:T(1024)S(1)} %add_rsqrt_fusion.1), kind=kOutput, calls=%fused_computation.31 | convolution fusion | flops 51415547904 | bytes 75985920 | tf_op jit(solution)/shard_map/dot_general | solution.py:65
  627.9 63.8 %convolution_convert_fusion = bf16[2304,5120]{1,0:T(8,128)(2,1)} fusion(bf16[2304,2176]{1,0:T(8,128)(2,1)} %fusion.19, bf16[2176,5120]{1,0:T(8,128)(2,1)} %param.27), kind=kOutput, calls=%fused_computation.21 | convolution fusion | flops 51350077440 | bytes 55902208 | tf_op jit(solution)/shard_map/dot_general | solution.py:67
  691.7 1.0 copy-done.2
  693.1 1.5 select_bitcast_fusion
  694.5 287.2 %all-reduce.5.cloned.1.call-done = bf16[2304,5120]{1,0:T(8,128)(2,1)} async-done(((bf16[2304,5120]{1,0:T(8,128)(2,1)}), bf16[2304,5120]{1,0:T(8,128)(2,1)}) %all-reduce.5.cloned.1.call-update) | async-done | bytes 23592976 | tf_op jit(solution)/shard_map/psum | solution.py:68
  981.7 26.8 %fusion.4 = bf16[2304,5120]{1,0:T(8,128)(2,1)} fusion(bf16[2304,5120]{1,0:T(8,128)(2,1)} %get-tuple-element.10, bf16[2304,5120]{1,0:T(8,128)(2,1)} %all-reduce.5.cloned.1.call-done), kind=kLoop, calls=%fused_computation.7 | loop fusion | flops 47185920 | bytes 70778880 | tf_op jit(solution)/shard_map/convert_element_type | solution.py:69
  (43 shorter events, 5.6 us)
Async XLA Ops:
  7.2 13.0 %copy-start.10 = (bf16[5120]{0:T(1024)(128)(2,1)S(1)}, bf16[5120]{0:T(1024)(128)(2,1)}, u32[]{:S(2)}) copy-start(bf16[5120]{0:T(1024)(128)(2,1)} %param.17) | copy-start | bytes 30724
  7.2 458.7 %all-reduce.3.cloned.1.call-start = ((), (), s32[]{:S(2)}) async-start(), calls=%async_computation | async-start | bytes 47185920 | tf_op jit(solution)/shard_map/psum | solution.py:61
  9.5 95.2 %copy-start.8 = (pred[3,768]{1,0:T(4,128)(4,1)}, pred[3,768]{1,0:T(4,128)(4,1)S(1)}, u32[]{:S(2)}) copy-start(pred[3,768]{1,0:T(4,128)(4,1)S(1)} %iota_compare_fusion.1) | copy-start | bytes 6916
  74.1 15.0 %copy-start = (bf16[2304,5120]{1,0:T(8,128)(2,1)S(1)}, bf16[2304,5120]{1,0:T(8,128)(2,1)}, u32[]{:S(2)}) copy-start(bf16[2304,5120]{1,0:T(8,128)(2,1)} %fusion.9) | copy-start | bytes 70778880
  104.7 27.1 %copy-start.1 = (bf16[3,768,1,64]{3,1,0,2:T(8,128)(2,1)}, bf16[3,768,1,64]{3,1,0,2:T(8,128)(2,1)S(1)}, u32[]{:S(2)}) copy-start(bf16[3,768,1,64]{3,1,0,2:T(8,128)(2,1)S(1)} %get-tuple-element.13) | copy-start | bytes 884740
  104.7 27.1 %copy-start.3 = (bf16[3,768,1,64]{3,1,0,2:T(8,128)(2,1)}, bf16[3,768,1,64]{3,1,0,2:T(8,128)(2,1)S(1)}, u32[]{:S(2)}) copy-start(bf16[3,768,1,64]{3,1,0,2:T(8,128)(2,1)S(1)} %get-tuple-element.14) | copy-start | bytes 884740
  106.6 6.3 copy-start.5
  112.9 18.9 %copy-start.6 = (bf16[2304,128]{1,0:T(8,128)(2,1)S(1)}, bf16[2304,128]{1,0:T(8,128)(2,1)}, u32[]{:S(2)}) copy-start(bf16[2304,128]{1,0:T(8,128)(2,1)} %convolution_convert_fusion.2) | copy-start | bytes 1769476
  173.2 0.7 copy-start.11
  173.2 808.5 %all-reduce.5.cloned.1.call-start = ((), (), s32[]{:S(2)}) async-start(), calls=%async_computation.1 | async-start | bytes 47185920 | tf_op jit(solution)/shard_map/psum | solution.py:68
  691.7 1.1 copy-start.2
  691.7 1.2 copy-start.4
  691.7 1.4 copy-start.7
  691.7 1.4 copy-start.9
Sparse Core Ops, SparseCore 0:
  173.3 292.4 all-reduce.2
  691.8 289.8 all-reduce.4
where the time goes:
time: 1020 us
  waiting for transfers between devices  579 us (57%)
  matrix products  300 us (29%)
  other arithmetic  107 us (10%)
  local copies, waits for them, and re-layouts  15.1 us (1%)
  between operations  14.4 us (1%)
    psum x1, waiting for transfers between devices, layer_body(): attn_sum = lax.psum(attn_part, 'tp')  292 us
    psum x1, waiting for transfers between devices, layer_body(): mlp_sum = lax.psum(mlp_part, 'tp')  287 us
    dot_general x1, matrix products, layer_body(): up_proj = jnp.dot(normed_mlp, w_up, preferred_element_type=jnp.float32)  67.6 us
    dot_general x1, matrix products, layer_body(): gate_proj = jnp.dot(normed_mlp, w_gate, preferred_element_type=jnp.float32)  66.4 us
    dot_general x1, matrix products, layer_body(): jnp.dot(gated, w_down, preferred_element_type=jnp.float32)  63.8 us
    reduce_sum x2, other arithmetic, rms_scale(): mean_sq = jnp.mean(values * values, axis=-1, keepdims=True)  38 us
    convert_element_type x1, other arithmetic, layer_body(): (hidden + mlp_sum.astype(jnp.float32)).astype(jnp.bfloat16)  26.8 us
    dot_general x1, matrix products, layer_body(): jnp.dot(attn_rows, w_out, preferred_element_type=jnp.float32)  25.4 us
  transfers between devices with their start and end apart: 2, of which 2 were waited for; matrix products, arithmetic and copies ran while one was open for 0% of the time, Pallas kernels for 0%

commit v1 on v0

v1 whole, which is shorter than its diff:
```python
import functools
import jax
import jax.numpy as jnp
from jax import lax
from jax.experimental import pallas as pl
from jax.experimental.pallas import tpu as pltpu
from jax.sharding import PartitionSpec as P

EPSILON = 1e-6
ROPE_THETA = 1000000.0
MESH = pl.DeviceIdType.MESH
F32, BF16 = jnp.float32, jnp.bfloat16
SLOTS = ((0, 0, 0), (0, 1, 0), (0, 0, 1), (0, 1, 1), (1, 0, 0), (1, 0, 1), (1, 1, 0), (1, 1, 1))


def rms_scale(values, gain_vec):
    mean_sq = jnp.mean(values * values, axis=-1, keepdims=True)
    return values * lax.rsqrt(mean_sq + EPSILON) * gain_vec.astype(F32)


def rope_tables(positions, half_dim):
    inv_freq = ROPE_THETA ** (-jnp.arange(half_dim, dtype=F32) / half_dim)
    angles = positions.astype(F32)[:, :, None] * inv_freq
    return jnp.cos(angles)[:, :, None, :], jnp.sin(angles)[:, :, None, :]


def rope_apply(values, cosine, sine_tab):
    half_dim = values.shape[-1] // 2
    first_half = values[..., :half_dim]
    second_half = values[..., half_dim:]
    return jnp.concatenate([first_half * cosine - second_half * sine_tab, second_half * cosine + first_half * sine_tab], axis=-1)


def local_attention(q_rot, k_rot, v_vals, lengths):
    seq_len, head_dim = k_rot.shape[1], k_rot.shape[2]
    scores = jnp.einsum('bshd,btd->bhst', q_rot, k_rot, preferred_element_type=F32) * head_dim ** -0.5
    row_idx = jnp.arange(seq_len)[:, None]
    col_idx = jnp.arange(seq_len)[None, :]
    allowed = (col_idx <= row_idx)[None, None] & (col_idx[None, None] < lengths[:, None, None, None])
    attn_probs = jax.nn.softmax(jnp.where(allowed, scores, -1e30), axis=-1).astype(BF16)
    return jnp.einsum('bhst,btd->bshd', attn_probs, v_vals, preferred_element_type=F32).astype(BF16)


def flip(t, bit):
    return t + bit - 2 * bit * lax.rem(lax.div(t, bit), 2)


def origin_block(t, slot):
    part, dy, dx = SLOTS[slot % 8]
    owner = t
    if slot >= 8:
        owner = flip(owner, 1)
    if dx:
        owner = flip(owner, 2)
    if dy:
        owner = flip(owner, 4)
    return 2 * owner + part


def stage_kernel(cfg, *refs):
    kind, ars, steps, width, rows, ffn_tile = cfg['kind'], cfg['ars'], cfg['steps'], cfg['width'], cfg['rows'], cfg['ffn_tile']
    piece = rows // 16
    half = rows // 2
    quarter = rows // 8
    it = iter(refs)
    take = lambda: next(it)
    n_chunks = len(cfg['chunks'])
    if kind == 'mlp':
        lhs_hbm, wg_hbm, wu_hbm, wd_ref = take(), take(), take(), take()
    elif kind == 'wout':
        lhs_hbm, wo_ref = take(), take()
    ar_in = []
    for ar in ars:
        d = dict(own=take(), rcv=take(), res=take())
        if ar['kind'] == 'attn':
            d['gain'] = take()
        ar_in.append(d)
    out_own, out_rcv = [], []
    for _ in range(n_chunks):
        out_own.append(take())
        out_rcv.append(take())
    for d, ar in zip(ar_in, ars):
        d['g'] = take()
        if ar['kind'] == 'attn':
            d['h'] = take()
    if kind == 'mlp':
        lhs, gated, wbuf, w_sem = take(), take(), take(), take()
    elif kind == 'wout':
        lhs = take()
    if n_chunks:
        obuf, lhs_sem, o_sem, os_sem, or_sem = take(), take(), take(), take(), take()
    for d, ar in zip(ar_in, ars):
        for name in ('s', 'r', 'r1', 'r2', 'x', 'n', 'send', 'recv', 'loc'):
            d[name] = take()

    t = lax.axis_index('tp')
    core, xn, yn = {'tp': flip(t, 1)}, {'tp': flip(t, 2)}, {'tp': flip(t, 4)}
    step = pl.program_id(0)

    def rcopy(d, i, src, dst, dev):
        return pltpu.make_async_remote_copy(src_ref=src, dst_ref=dst, send_sem=d['send'].at[i], recv_sem=d['recv'].at[i], device_id=dev, device_id_type=MESH)

    def lcopy(sem, src, dst):
        return pltpu.make_async_copy(src, dst, sem)

    def at(ref, start, n):
        return ref.at[pl.ds(start, n)]

    def slots(d, first, n=1):
        return at(d['g'], first * piece, n * piece)

    def ar_loads(d, ar):
        if ar['kind'] == 'attn':
            res = at(d['res'], ar['chunk'] * rows + pl.multiple_of(t * quarter, quarter), quarter)
        else:
            res = d['res']
        return [lcopy(d['loc'].at[0], d['own'], d['s']), lcopy(d['loc'].at[1], d['rcv'], d['r']), lcopy(d['loc'].at[2], res, d['x'])]

    def p1(d):
        return [rcopy(d, 0, at(d['s'], quarter, quarter), d['r1'].at[0], xn), rcopy(d, 1, at(d['s'], 3 * quarter, quarter), d['r1'].at[1], yn)]

    def p2(d):
        return [rcopy(d, 2, at(d['s'], piece, piece), d['r2'].at[0], yn), rcopy(d, 3, at(d['s'], 2 * quarter + piece, piece), d['r2'].at[1], xn)]

    def p3(d):
        a, b = at(d['n'], 0, piece), at(d['n'], piece, piece)
        return [rcopy(d, 4, a, slots(d, 1), yn), rcopy(d, 5, b, slots(d, 5), xn), rcopy(d, 6, a, slots(d, 2), xn), rcopy(d, 7, b, slots(d, 6), yn),
                rcopy(d, 10, a, slots(d, 8), core), rcopy(d, 11, b, slots(d, 12), core)]

    def own_out(d):
        return [lcopy(d['loc'].at[3], at(d['n'], 0, piece), slots(d, 0)), lcopy(d['loc'].at[4], at(d['n'], piece, piece), slots(d, 4))]

    def h_out(d):
        return lcopy(d['loc'].at[5], d['x'], d['h'])

    def p4(d):
        return [rcopy(d, 8, slots(d, 1), slots(d, 3), xn), rcopy(d, 9, slots(d, 5), slots(d, 7), yn)]

    def c1(d):
        return [rcopy(d, 12, slots(d, 1, 2), slots(d, 9, 2), core), rcopy(d, 13, slots(d, 5, 2), slots(d, 13, 2), core)]

    def c2(d):
        return [rcopy(d, 14, slots(d, 3), slots(d, 11), core), rcopy(d, 15, slots(d, 7), slots(d, 15), core)]

    def add_rows(dst, dst0, src, src0, n):
        def body(i, _):
            a = pl.ds(pl.multiple_of(dst0 + i * 16, 16), 16)
            b = pl.ds(pl.multiple_of(src0 + i * 16, 16), 16)
            dst[a, :] = (dst[a, :].astype(F32) + src[b, :].astype(F32)).astype(BF16)
            return 0
        lax.fori_loop(0, n // 16, body, 0)

    def ar_start_loads():
        for d, ar in zip(ar_in, ars):
            for cp in ar_loads(d, ar):
                cp.start()

    def ar_phase1():
        for d, ar in zip(ar_in, ars):
            for cp in ar_loads(d, ar):
                cp.wait()
            add_rows(d['s'], quarter, d['r'], quarter, quarter)
            p1(d)[0].start()
            add_rows(d['s'], 3 * quarter, d['r'], 3 * quarter, quarter)
            p1(d)[1].start()
            add_rows(d['s'], 0, d['r'], 0, quarter)
            add_rows(d['s'], 2 * quarter, d['r'], 2 * quarter, quarter)

    def ar_phase2():
        for d in ar_in:
            a, b = p1(d)
            a.wait_recv()
            add_rows(d['s'], piece, d['r1'].at[0], piece, piece)
            p2(d)[0].start()
            b.wait_recv()
            add_rows(d['s'], 2 * quarter + piece, d['r1'].at[1], piece, piece)
            p2(d)[1].start()
            add_rows(d['s'], 0, d['r1'].at[0], 0, piece)
            add_rows(d['s'], 2 * quarter, d['r1'].at[1], 0, piece)

    def ar_finish(d, ar, part):
        base = part * piece
        src0 = part * 2 * quarter

        def body(i, _):
            here = pl.ds(pl.multiple_of(base + i * 16, 16), 16)
            there = pl.ds(pl.multiple_of(src0 + i * 16, 16), 16)
            other = pl.ds(pl.multiple_of(i * 16, 16), 16)
            total = d['s'][there, :].astype(F32) + d['r2'][part, other, :].astype(F32)
            hid = (d['x'][here, :].astype(F32) + total).astype(BF16)
            if ar['kind'] == 'attn':
                d['x'][here, :] = hid
                hid = hid.astype(F32)
                mean_sq = jnp.sum(hid * hid, axis=-1, keepdims=True) / width
                hid = (hid * lax.rsqrt(mean_sq + EPSILON) * d['gain'][...].astype(F32)).astype(BF16)
            d['n'][here, :] = hid
            return 0
        lax.fori_loop(0, piece // 16, body, 0)

    def ar_phase3():
        for d, ar in zip(ar_in, ars):
            cps = p3(d)
            rec = p2(d)
            rec[0].wait_recv()
            ar_finish(d, ar, 0)
            cps[0].start()
            rec[1].wait_recv()
            ar_finish(d, ar, 1)
            for cp in cps[1:]:
                cp.start()
            for cp in own_out(d):
                cp.start()
            if ar['kind'] == 'attn':
                h_out(d).start()

    def ar_phase4():
        for d in ar_in:
            cps = p3(d)
            fwd = p4(d)
            cps[0].wait_recv()
            fwd[0].start()
            cps[1].wait_recv()
            fwd[1].start()

    def ar_end():
        for d in ar_in:
            cps, cc = p3(d), c1(d)
            cps[2].wait_recv()
            cc[0].start()
            cps[3].wait_recv()
            cc[1].start()
        for d in ar_in:
            fwd, cc = p4(d), c2(d)
            fwd[0].wait_recv()
            cc[0].start()
            fwd[1].wait_recv()
            cc[1].start()
        for d, ar in zip(ar_in, ars):
            cps = p3(d)
            cps[4].wait_recv()
            cps[5].wait_recv()
            for cp in c1(d) + c2(d):
                cp.wait_recv()
            for cp in p1(d) + p2(d) + p3(d) + p4(d) + c1(d) + c2(d):
                cp.wait_send()
            for cp in own_out(d):
                cp.wait()
            if ar['kind'] == 'attn':
                h_out(d).wait()

    def w_copies(j):
        slot = lax.rem(j, 2)
        cols = pl.ds(pl.multiple_of(j * ffn_tile, ffn_tile), ffn_tile)
        return [lcopy(w_sem.at[slot, 0], wg_hbm.at[:, cols], wbuf.at[slot, :, pl.ds(0, ffn_tile)]),
                lcopy(w_sem.at[slot, 1], wu_hbm.at[:, cols], wbuf.at[slot, :, pl.ds(ffn_tile, ffn_tile)])]

    def lhs_copies():
        if kind == 'mlp':
            return [lcopy(lhs_sem.at[0], lhs_hbm, lhs)]
        out = []
        for ci, chunk in enumerate(cfg['chunks']):
            for s in range(16):
                src = at(lhs_hbm, chunk * rows + pl.multiple_of(origin_block(t, s) * piece, piece), piece)
                out.append(lcopy(lhs_sem.at[ci * 16 + s], src, lhs.at[ci, pl.ds(s * piece, piece)]))
        return out

    def tile_copies(ci, j, slot):
        n = obuf.shape[2]
        cols = pl.ds(pl.multiple_of(j * n, n), n)
        return (lcopy(o_sem.at[slot], obuf.at[slot, pl.ds(0, half)], out_own[ci].at[:, cols]),
                pltpu.make_async_remote_copy(src_ref=obuf.at[slot, pl.ds(half, half)], dst_ref=out_rcv[ci].at[:, cols],
                                             send_sem=os_sem.at[slot], recv_sem=or_sem.at[ci], device_id=core, device_id_type=MESH))

    n_steps = cfg['n_steps']

    @pl.when(step == 0)
    def _():
        ar_start_loads()
        if n_chunks:
            for cp in lhs_copies():
                cp.start()
        if kind == 'mlp':
            for cp in w_copies(0):
                cp.start()
        barrier = pltpu.get_barrier_semaphore()
        for dev in (core, xn, yn):
            pl.semaphore_signal(barrier, inc=1, device_id=dev, device_id_type=MESH)
        pl.semaphore_wait(barrier, 3)
        ar_phase1()
        if n_chunks:
            for cp in lhs_copies():
                cp.wait()

    if ars:
        for at_step, phase in zip(steps, (ar_phase2, ar_phase3, ar_phase4)):
            pl.when(step == at_step)(phase)

    def store_tile(ci, j, count, value):
        slot = lax.rem(count, 2)

        @pl.when(count >= 2)
        def _():
            a, b = tile_copies(ci, j, slot)
            a.wait()
            b.wait_send()
        obuf[slot] = value
        a, b = tile_copies(ci, j, slot)
        a.start()
        b.start()

    if kind == 'mlp':
        n_up = cfg['n_up']

        @pl.when(step < n_up)
        def _():
            @pl.when(step + 1 < n_up)
            def _():
                for cp in w_copies(step + 1):
                    cp.start()
            for cp in w_copies(step):
                cp.wait()
            both = jnp.dot(lhs[...], wbuf[lax.rem(step, 2)], preferred_element_type=F32)
            gate = both[:, :ffn_tile]
            gated[:, pl.ds(pl.multiple_of(step * ffn_tile, ffn_tile), ffn_tile)] = (gate * jax.nn.sigmoid(gate) * both[:, ffn_tile:]).astype(BF16)

        @pl.when(step >= n_up)
        def _():
            store_tile(0, step - n_up, step - n_up, jnp.dot(gated[...], wd_ref[...], preferred_element_type=F32).astype(BF16))
    elif kind == 'wout':
        per = cfg['per']
        for ci in range(n_chunks):
            @pl.when(lax.div(step, per) == ci)
            def _(ci=ci):
                store_tile(ci, step - ci * per, step, jnp.dot(lhs[ci], wo_ref[...], preferred_element_type=F32).astype(BF16))

    @pl.when(step == n_steps - 1)
    def _():
        if n_chunks:
            per = cfg['per']
            for j in (per - 2, per - 1):
                a, b = tile_copies(n_chunks - 1, j, ((n_chunks - 1) * per + j) % 2)
                a.wait()
                b.wait_send()
            for ci in range(n_chunks):
                pltpu.make_async_copy(out_rcv[ci], out_rcv[ci], or_sem.at[ci]).wait()
        ar_end()


def run_stage(cid, kind, compute, ars, steps, rows, width, chunks=()):
    any_spec = pl.BlockSpec(memory_space=pl.ANY)
    half, quarter, piece = rows // 2, rows // 8, rows // 16
    args, in_specs, out_shape, scratch = [], [], [], []
    out_tile = 512 if width % 512 == 0 else 128
    per = width // out_tile
    cfg = dict(kind=kind, steps=steps, width=width, rows=rows, chunks=chunks, per=per, ffn_tile=128,
               ars=[dict(kind=a['kind'], chunk=a['chunk']) for a in ars])
    if kind == 'mlp':
        n2, wg, wu, wd = compute
        ffn = wd.shape[0]
        n_up = ffn // 128
        cfg.update(n_up=n_up, n_steps=n_up + per)
        args += [n2, wg, wu, wd]
        in_specs += [any_spec] * 3 + [pl.BlockSpec((ffn, out_tile), lambda j: (0, jnp.maximum(j - n_up, 0)))]
        scratch += [pltpu.VMEM((rows, width), BF16), pltpu.VMEM((rows, ffn), BF16), pltpu.VMEM((2, width, 256), BF16), pltpu.SemaphoreType.DMA((2, 2))]
        n_lhs = 1
    elif kind == 'wout':
        o, wo = compute
        cfg.update(n_steps=per * len(chunks))
        args += [o, wo]
        in_specs += [any_spec, pl.BlockSpec((wo.shape[0], out_tile), lambda j: (0, lax.rem(j, per)))]
        scratch += [pltpu.VMEM((len(chunks), rows, wo.shape[0]), BF16)]
        n_lhs = 16 * len(chunks)
    else:
        cfg.update(n_steps=max(steps) + 1)
    if chunks:
        scratch += [pltpu.VMEM((2, rows, out_tile), BF16), pltpu.SemaphoreType.DMA((n_lhs,)), pltpu.SemaphoreType.DMA((2,)),
                    pltpu.SemaphoreType.DMA((2,)), pltpu.SemaphoreType.DMA((len(chunks),))]
    for a in ars:
        args += [a['own'], a['rcv'], a['res']]
        in_specs += [any_spec] * 3
        if a['kind'] == 'attn':
            args.append(a['gain'])
            in_specs.append(pl.BlockSpec((1, width), lambda j: (0, 0)))
        scratch += [pltpu.VMEM((half, width), BF16), pltpu.VMEM((half, width), BF16), pltpu.VMEM((2, quarter, width), BF16),
                    pltpu.VMEM((2, piece, width), BF16), pltpu.VMEM((quarter, width), BF16), pltpu.VMEM((quarter, width), BF16),
                    pltpu.SemaphoreType.DMA((16,)), pltpu.SemaphoreType.DMA((16,)), pltpu.SemaphoreType.DMA((6,))]
    for _ in chunks:
        out_shape += [jax.ShapeDtypeStruct((half, width), BF16)] * 2
    for a in ars:
        out_shape.append(jax.ShapeDtypeStruct((rows, width), BF16))
        if a['kind'] == 'attn':
            out_shape.append(jax.ShapeDtypeStruct((quarter, width), BF16))
    return pl.pallas_call(
        functools.partial(stage_kernel, cfg),
        grid=(cfg['n_steps'],),
        out_shape=out_shape,
        in_specs=in_specs,
        out_specs=[any_spec] * len(out_shape),
        scratch_shapes=scratch,
        compiler_params=pltpu.CompilerParams(collective_id=cid, has_side_effects=True, vmem_limit_bytes=62 * 1024 * 1024,
                                             dimension_semantics=('arbitrary',)),
        name=f'stage{cid}',
    )(*args)


def place_kernel(n, table_ref, *refs):
    for b in range(n):
        refs[n][b] = refs[b][...]


def place_rows(chunks, rows, width):
    t = lax.axis_index('tp')
    piece = rows // 16
    blocks = jnp.stack([jnp.asarray(origin_block(t, s), jnp.int32) for s in range(16)])
    table = jnp.argmax(blocks[None, :] == jnp.arange(16, dtype=jnp.int32)[:, None], axis=1).astype(jnp.int32)
    n = len(chunks)
    return pl.pallas_call(
        functools.partial(place_kernel, n),
        grid_spec=pltpu.PrefetchScalarGridSpec(
            num_scalar_prefetch=1, grid=(16,),
            in_specs=[pl.BlockSpec((piece, width), lambda k, tab: (tab[k], 0))] * n,
            out_specs=pl.BlockSpec((n, piece, width), lambda k, tab: (0, k, 0))),
        out_shape=jax.ShapeDtypeStruct((n, rows, width), BF16),
        name='place',
    )(table, *chunks)


def layer_body(tokens, positions, lengths, norm_attn, norm_mlp, q_gain, k_gain, w_query, w_key, w_value, w_out, w_gate, w_up, w_down, tp_size):
    num_prompts, seq_len, hidden_dim = tokens.shape
    head_dim = q_gain.shape[0]
    local_heads = w_query.shape[1] // head_dim
    kv_heads = w_key.shape[1] // head_dim
    kv_index = lax.axis_index('tp') // (tp_size // kv_heads)
    rows_n = num_prompts * seq_len
    tokens_flat = tokens.reshape(rows_n, hidden_dim)
    normed = rms_scale(tokens_flat.astype(F32), norm_attn).astype(BF16)
    w_key_head = lax.dynamic_slice_in_dim(w_key, kv_index * head_dim, head_dim, axis=1)
    w_value_head = lax.dynamic_slice_in_dim(w_value, kv_index * head_dim, head_dim, axis=1)
    q_proj = jnp.dot(normed, w_query, preferred_element_type=F32).reshape(num_prompts, seq_len, local_heads, head_dim)
    k_proj = jnp.dot(normed, w_key_head, preferred_element_type=F32).reshape(num_prompts, seq_len, 1, head_dim)
    v_vals = jnp.dot(normed, w_value_head, preferred_element_type=F32).astype(BF16).reshape(num_prompts, seq_len, head_dim)
    cosine, sine_tab = rope_tables(positions, head_dim // 2)
    q_rot = rope_apply(rms_scale(q_proj, q_gain), cosine, sine_tab).astype(BF16)
    k_rot = rope_apply(rms_scale(k_proj, k_gain), cosine, sine_tab).astype(BF16).reshape(num_prompts, seq_len, head_dim)
    valid_mask = (jnp.arange(seq_len)[None, :] < lengths[:, None])[:, :, None]
    k_cache = jnp.where(valid_mask, k_rot, 0).astype(BF16)[:, :, None, :]
    v_cache = jnp.where(valid_mask, v_vals, 0).astype(BF16)[:, :, None, :]
    attn_rows = local_attention(q_rot, k_rot, v_vals, lengths).reshape(rows_n, local_heads * head_dim)

    gain = norm_mlp.reshape(1, hidden_dim)
    stage = functools.partial(run_stage, rows=seq_len, width=hidden_dim)

    def attn_ar(chunk, own, rcv):
        return dict(kind='attn', chunk=chunk, own=own, rcv=rcv, res=tokens_flat, gain=gain)

    def mlp_ar(own, rcv, hid):
        return dict(kind='mlp', chunk=0, own=own, rcv=rcv, res=hid)

    weights = (w_gate, w_up, w_down)
    own0, rcv0 = stage(1, 'wout', (attn_rows, w_out), [], (), chunks=(0,))
    own1, rcv1, own2, rcv2, n0, h0 = stage(2, 'wout', (attn_rows, w_out), [attn_ar(0, own0, rcv0)], (17, 18, 19), chunks=(1, 2))
    m_own0, m_rcv0, n1, h1 = stage(3, 'mlp', (n0, *weights), [attn_ar(1, own1, rcv1)], (11, 16, 22), chunks=(0,))
    m_own1, m_rcv1, n2, h2, out0 = stage(4, 'mlp', (n1, *weights), [attn_ar(2, own2, rcv2), mlp_ar(m_own0, m_rcv0, h0)], (20, 25, 26), chunks=(1,))
    m_own2, m_rcv2, out1 = stage(5, 'mlp', (n2, *weights), [mlp_ar(m_own1, m_rcv1, h1)], (11, 16, 22), chunks=(2,))
    out2, = stage(6, 'none', (), [mlp_ar(m_own2, m_rcv2, h2)], (0, 1, 2))
    output = place_rows([out0, out1, out2], seq_len, hidden_dim)
    return output, k_cache, v_cache


def solution(mesh):
    body = functools.partial(layer_body, tp_size=mesh.shape['tp'])
    in_specs = (P('dp', None, None), P('dp', None), P('dp'), P(), P(), P(), P(), P(None, 'tp'), P(), P(), P('tp', None), P(None, 'tp'), P(None, 'tp'), P('tp', None))
    out_specs = (P('dp', None, None), P('dp', None, 'tp', None), P('dp', None, 'tp', None))
    return jax.shard_map(body, mesh=mesh, in_specs=in_specs, out_specs=out_specs, check_vma=False)
```

time: 1020 us -> 645 us (0.63)
  waiting for transfers between devices: 579 us -> 0 us
  Pallas kernels: 0 us -> 506 us
  matrix products: 300 us -> 77.1 us
  other arithmetic: 107 us -> 30.5 us
  between operations: 14.4 us -> 1.39 us
    psum x2 -> x0, waiting for transfers between devices: 579 us -> none  [the longest x1 292 us: layer_body(): attn_sum = lax.psum(attn_part, 'tp')]
    pallas_call x0 -> x7, Pallas kernels: none -> 506 us  [the longest x6 484 us: run_stage(): pl.pallas_call(functools.partial(stage_kernel, cfg), grid=(cfg['n_steps']...]
    dot_general x8 -> x4, matrix products: 281 us -> 58.2 us  [the longest x1 21.8 us: layer_body(): jnp.dot(normed, w_query, preferred_element_type=F32)]
    convert_element_type x7 -> x4, other arithmetic: 50.6 us -> 2.54 us  [the longest x3 1.83 us: rms_scale(): return values * lax.rsqrt(mean_sq + EPSILON) * gain_vec.astype(F32)]
    reduce_sum x2 -> x1, other arithmetic: 38 us -> 9.97 us  [rms_scale(): mean_sq = jnp.mean(values * values, axis=-1, keepdims=True)]
  transfers between devices with their start and end apart: 2 -> 0, of which waited for: 2 -> 0; matrix products, arithmetic and copies ran while one was open for 0% -> 0% of each run, Pallas kernels for 0% -> 0%
where the time goes in v1:
time: 645 us; the launch traced here: 635 us
  Pallas kernels  506 us (78%)
  matrix products  77.1 us (12%)
  other arithmetic  30.5 us (5%)
  local copies, waits for them, and re-layouts  19.7 us (3%)
    pallas_call x6, Pallas kernels, run_stage(): pl.pallas_call(functools.partial(stage_kernel, cfg), grid=(cfg['n_steps']...  484 us
    dot_general x1, matrix products, layer_body(): jnp.dot(normed, w_query, preferred_element_type=F32)  21.8 us
    pallas_call x1, Pallas kernels, place_rows(): pl.pallas_call(functools.partial(place_kernel, n), grid_spec=pltpu.Prefet...  21.7 us
    sub x1, matrix products, local_attention(): jax.nn.softmax(jnp.where(allowed, scores, -1e+30), axis=-1).astype(BF16)  18.9 us
    unnamed x16, local copies, waits for them, and re-layouts  14.4 us
    dot_general x1, matrix products, local_attention(): jnp.einsum('bhst,btd->bshd', attn_probs, v_vals, preferred_element_type=F32)  13 us

profile of v1, /device:TPU:0, one launch (start us, length us, event | category | flops | bytes accessed | tf_op | source)
XLA Modules:
  0.0 634.8 jit_solution(5825088447104574477)
XLA Ops:
  1.4 1.2 convert_element_type.60
  3.9 0.7 iota_compare_fusion.1
  5.3 10.0 %fusion.1 = f32[3,768]{1,0:T(4,128)S(1)} fusion(bf16[3,768,5120]{2,1,0:T(8,128)(2,1)} %param.14), kind=kLoop, calls=%fused_computation.3 | loop fusion | flops 35387136 | bytes 23602176 | tf_op jit(solution)/shard_map/reduce_sum | solution.py:17
  16.0 11.7 %fusion.16 = bf16[2304,128]{1,0:T(8,128)(2,1)S(1)} fusion(bf16[2304,5120]{1,0:T(8,128)(2,1)} %bitcast.74, f32[5120]{0:T(1024)S(1)} %convert_element_type.54, f32[2304]{0:T(1024)S(1)} %rsqrt.32, bf16[5120,1024]{1,0:T(8,128)(2,1)} %param.23, s32[]{:T(128)S(6)} %select_n.36), kind=kOutput, calls=%fused_computation.22 | convolution fusion | flops 3067379712 | bytes 25523204 | tf_op jit(solution)/shard_map/dot_general | solution.py:441
  27.9 11.8 %multiply_reduce_fusion.1 = (f32[2304]{0:T(1024)S(1)}, f32[2304,128]{1,0:T(8,128)S(1)}) fusion(bf16[5120,1024]{1,0:T(8,128)(2,1)} %param.22, s32[]{:T(128)S(6)} %select_n.36, bf16[2304,5120]{1,0:T(8,128)(2,1)} %bitcast.75, f32[5120]{0:T(1024)S(1)} %convert_element_type.54, f32[2304]{0:T(1024)S(1)} %rsqrt.32), kind=kOutput, calls=%fused_computation.44 | convolution fusion | flops 3067672320 | bytes 26122244 | tf_op jit(solution)/shard_map/dot_general | solution.py:440
  40.1 5.9 fusion.25
  46.0 2.8 multiply_cosine_fusion.1
  48.8 1.9 broadcast_and_fusion
  50.7 1.5 select_bitcast_fusion
  52.2 9.7 %copy.33 = bf16[5120,640]{0,1:T(8,128)(2,1)} copy(bf16[5120,640]{1,0:T(8,128)(2,1)} %param.21) | data formatting | bytes 13107200 | tf_op args[7]
  61.9 21.8 %multiply_reduce_fusion = (f32[3,768,5]{1,2,0:T(8,128)S(1)}, f32[3,768,5,128]{1,3,2,0:T(8,128)S(1)}) fusion(bf16[5,128,5120,1]{2,1,0,3:T(8,128)(2,1)} %bitcast.82, bf16[3,768,5120]{2,1,0:T(8,128)(2,1)} %param.14, f32[5120]{0:T(1024)S(1)} %copy-done.3, f32[3,768]{1,0:T(4,128)S(1)} %copy-done.1), kind=kOutput, calls=%fused_computation.21 | convolution fusion | flops 15149618176 | bytes 36120576 | tf_op jit(solution)/shard_map/dot_general | solution.py:439
  83.7 0.8 multiply_multiply_fusion
  84.5 2.6 subtract_convert_fusion
  87.1 18.9 %fusion.37 = (f32[3,5,768]{2,1,0:T(8,128)}, f32[3,5,768,768]{2,3,1,0:T(8,128)}) fusion(pred[3,768,768]{1,2,0:T(8,128)(4,1)} %broadcast_and_fusion, bf16[3,768,5,64]{1,3,2,0:T(8,128)(2,1)} %get-tuple-element.55, bf16[3,768,5,64]{1,3,2,0:T(8,128)(2,1)} %get-tuple-element.54, bf16[3,768,64]{2,1,0:T(8,128)(2,1)S(1)} %bitcast.84, ...), kind=kOutput, calls=%fused_computation.64 | convolution fusion | flops 2307392256 | bytes 40743936 | tf_op jit(solution)/shard_map/sub | solution.py:40
  106.0 13.0 %convert_bitcast_fusion = bf16[3,768,5,128]{1,3,2,0:T(8,128)(2,1)S(1)} fusion(bf16[3,768,128,1]{2,1,3,0:T(8,128)(2,1)S(1)} %bitcast.87, f32[3,5,768,768]{2,3,1,0:T(8,128)} %get-tuple-element.67, f32[3,5,768]{2,1,0:T(8,128)} %get-tuple-element.66), kind=kOutput, calls=%fused_computation.26 | convolution fusion | flops 2284093440 | bytes 38974464 | tf_op jit(solution)/shard_map/bhst,btd->bshd/dot_general | solution.py:41
  119.0 4.6 copy.49
  123.6 4.6 copy.53
  128.2 16.0 %stage1.1 = (bf16[384,5120]{1,0:T(8,128)(2,1)}, bf16[384,5120]{1,0:T(8,128)(2,1)}) custom-call(bf16[2304,640]{1,0:T(8,128)(2,1)} %bitcast.79, bf16[640,5120]{1,0:T(8,128)(2,1)} %refs_1_.6), custom_call_target="tpu_custom_call" | custom-call | tf_op jit(solution)/shard_map/stage1/pallas_call | solution.py:393
  144.3 78.1 %stage2.1 = (bf16[384,5120]{1,0:T(8,128)(2,1)}, bf16[384,5120]{1,0:T(8,128)(2,1)}, bf16[384,5120]{1,0:T(8,128)(2,1)}, bf16[384,5120]{1,0:T(8,128)(2,1)}, bf16[76...) custom-call(bf16[2304,640]{1,0:T(8,128)(2,1)} %bitcast.80, bf16[640,5120]{1,0:T(8,128)(2,1)} %refs_1_.6, ...), custom_call_target="tpu_custom_call" | custom-call | tf_op jit(solution)/shard_map/stage2/pallas_call | solution.py:393
  222.4 84.5 %stage3.1 = (bf16[384,5120]{1,0:T(8,128)(2,1)}, bf16[384,5120]{1,0:T(8,128)(2,1)}, bf16[768,5120]{1,0:T(8,128)(2,1)}, bf16[96,5120]{1,0:T(8,128)(2,1)}) custom-call(bf16[768,5120]{1,0:T(8,128)(2,1)} %get-tuple-element.27.refs_0_, bf16[5120,2176]{1,0:T(8,128)(2,1)} %refs_1_.9, bf16[5120,2176]{1,0:T(8,128)(2,1)} %refs_2_.5, bf16[2176,5120]{1,0:T(8,128)(2,1)} %refs_3_.5, ...), custom_call_target="tpu_custom_call" | custom-call | tf_op jit(solution)/shard_map/stage3/pallas_call | solution.py:393
  307.0 147.5 %stage4.1 = (bf16[384,5120]{1,0:T(8,128)(2,1)}, bf16[384,5120]{1,0:T(8,128)(2,1)}, bf16[768,5120]{1,0:T(8,128)(2,1)}, bf16[96,5120]{1,0:T(8,128)(2,1)}, bf16[768,5120]{1,0:T(8,128)(2,1)}) custom-call(bf16[768,5120]{1,0:T(8,128)(2,1)} %get-tuple-element.30.refs_0_, bf16[5120,2176]{1,0:T(8,128)(2,1)} %refs_1_.9, bf16[5120,2176]{1,0:T(8,128)(2,1)} %refs_2_.5, ...), custom_call_target="tpu_custom_call" | custom-call | tf_op jit(solution)/shard_map/stage4/pallas_call | solution.py:393
  454.5 83.1 %stage5.1 = (bf16[384,5120]{1,0:T(8,128)(2,1)}, bf16[384,5120]{1,0:T(8,128)(2,1)}, bf16[768,5120]{1,0:T(8,128)(2,1)}) custom-call(bf16[768,5120]{1,0:T(8,128)(2,1)} %get-tuple-element.37.refs_0_, bf16[5120,2176]{1,0:T(8,128)(2,1)} %refs_1_.9, bf16[5120,2176]{1,0:T(8,128)(2,1)} %refs_2_.5, bf16[2176,5120]{1,0:T(8,128)(2,1)} %refs_3_.5, ...), custom_call_target="tpu_custom_call" | custom-call | tf_op jit(solution)/shard_map/stage5/pallas_call | solution.py:393
  537.7 74.9 %stage6.1.refs_2_ = bf16[768,5120]{1,0:T(8,128)(2,1)} custom-call(bf16[384,5120]{1,0:T(8,128)(2,1)} %get-tuple-element.42.refs_0_, bf16[384,5120]{1,0:T(8,128)(2,1)} %get-tuple-element.43.refs_1_, bf16[96,5120]{1,0:T(8,128)(2,1)} %get-tuple-element.44.refs_2_), custom_call_target="tpu_custom_call" | custom-call | tf_op jit(solution)/shard_map/stage6/pallas_call | solution.py:393
  612.6 21.7 %place.1 = bf16[3,768,5120]{2,1,0:T(8,128)(2,1)} custom-call(s32[16]{0:T(128)} %get-tuple-element.24.table_ref, bf16[768,5120]{1,0:T(8,128)(2,1)} %get-tuple-element.36.refs_0_, bf16[768,5120]{1,0:T(8,128)(2,1)} %get-tuple-element.41.refs_1_, bf16[768,5120]{1,0:T(8,128)(2,1)} %stage6.1.refs_2_), custom_call_target="tpu_custom_call" | custom-call | tf_op jit(solution)/shard_map/place/pallas_call | solution.py:417
  (28 shorter events, 4.0 us)
Async XLA Ops:
  5.3 10.0 %copy-start.4 = (bf16[5120]{0:T(1024)(128)(2,1)S(1)}, bf16[5120]{0:T(1024)(128)(2,1)}, u32[]{:S(2)}) copy-start(bf16[5120]{0:T(1024)(128)(2,1)} %param.17) | copy-start | bytes 30724
  5.3 10.0 %copy-start.5 = (bf16[5120]{0:T(1024)(128)(2,1)S(1)}, bf16[5120]{0:T(1024)(128)(2,1)}, u32[]{:S(2)}) copy-start(bf16[5120]{0:T(1024)(128)(2,1)} %param.18) | copy-start | bytes 30724
  15.3 12.4 %copy-start = (f32[3,768]{1,0:T(4,128)}, f32[3,768]{1,0:T(4,128)S(1)}, u32[]{:S(2)}) copy-start(f32[3,768]{1,0:T(4,128)S(1)} %add_rsqrt_fusion.2) | copy-start | bytes 27652
  15.4 12.5 %copy-start.2 = (f32[5120]{0:T(1024)}, f32[5120]{0:T(1024)S(1)}, u32[]{:S(2)}) copy-start(f32[5120]{0:T(1024)S(1)} %convert_element_type.54) | copy-start | bytes 61444
  52.2 9.7 %copy-start.1 = (f32[3,768]{1,0:T(4,128)S(1)}, f32[3,768]{1,0:T(4,128)}, u32[]{:S(2)}) copy-start(f32[3,768]{1,0:T(4,128)} %copy-done) | copy-start | bytes 27652
  52.2 9.7 %copy-start.3 = (f32[5120]{0:T(1024)S(1)}, f32[5120]{0:T(1024)}, u32[]{:S(2)}) copy-start(f32[5120]{0:T(1024)} %copy-done.2) | copy-start | bytes 61444
  61.9 21.8 %copy-start.6 = (f32[128]{0:T(128)S(1)}, f32[128]{0:T(128)}, u32[]{:S(2)}) copy-start(f32[128]{0:T(128)} %convert_element_type.60) | copy-start | bytes 1540

commit v2 on v1

v2 whole, which is shorter than its diff:
```python
import functools
import jax
import jax.numpy as jnp
from jax import lax
from jax.experimental import pallas as pl
from jax.experimental.pallas import tpu as pltpu
from jax.sharding import PartitionSpec as P

EPSILON = 1e-6
ROPE_THETA = 1000000.0
MESH = pl.DeviceIdType.MESH
END = 1000
F32, BF16 = jnp.float32, jnp.bfloat16
SLOTS = ((0, 0, 0), (0, 1, 0), (0, 0, 1), (0, 1, 1), (1, 0, 0), (1, 0, 1), (1, 1, 0), (1, 1, 1))


def rope_tables(positions, half_dim):
    inv_freq = ROPE_THETA ** (-jnp.arange(half_dim, dtype=F32) / half_dim)
    angles = positions.astype(F32).reshape(-1, 1) * inv_freq
    cosine, sine = jnp.cos(angles), jnp.sin(angles)
    return jnp.concatenate([cosine, cosine], axis=-1), jnp.concatenate([-sine, sine], axis=-1)


class Lazy:
    def __init__(self, make):
        self.make = make

    def start(self):
        self.make().start()

    def wait(self):
        self.make().wait()

    def wait_send(self):
        self.make().wait_send()

    def wait_recv(self):
        self.make().wait_recv()


def flip(t, bit):
    return t + bit - 2 * bit * lax.rem(lax.div(t, bit), 2)


def origin_block(t, slot):
    part, dy, dx = SLOTS[slot % 8]
    owner = t
    if slot >= 8:
        owner = flip(owner, 1)
    if dx:
        owner = flip(owner, 2)
    if dy:
        owner = flip(owner, 4)
    return 2 * owner + part


def ar_scratch(do):
    return (() if do == 'ag' else ('s', 'r', 'r1', 'r2')) + (() if do == 'rs' else ('x',)) + ('n', 'send', 'recv', 'loc')


def stage_kernel(cfg, *refs):
    kind, ars, width, rows, ffn_tile = cfg['kind'], cfg['ars'], cfg['width'], cfg['rows'], cfg['ffn_tile']
    piece = rows // 16
    half = rows // 2
    quarter = rows // 8
    it = iter(refs)
    take = lambda: next(it)
    n_chunks = len(cfg['chunks'])
    if kind == 'mlp':
        lhs_hbm, wg_hbm, wu_hbm, wd_ref = take(), take(), take(), take()
    elif kind == 'head':
        len_ref, x_hbm, wq_hbm, wk_hbm, wv_hbm, norm_ref, qg_ref, kg_ref, cos_ref, sin_ref, wo_ref = (take() for _ in range(11))
    ar_in = []
    for ar in ars:
        d = {}
        if ar['do'] != 'ag' and ar['source'] is None:
            d.update(own=take(), rcv=take())
        if ar['do'] == 'ag':
            d['sum'] = take()
        if ar['do'] != 'rs':
            d['res'] = take()
            if ar['kind'] == 'attn':
                d['gain'] = take()
        ar_in.append(d)
    out_own, out_rcv = [], []
    for _ in range(n_chunks):
        out_own.append(take())
        out_rcv.append(take())
    if kind == 'head':
        kc_ref, vc_ref = take(), take()
    for d, ar in zip(ar_in, ars):
        if ar['source'] is not None:
            d.update(own=out_own[ar['source']], rcv=out_rcv[ar['source']])
        if ar['do'] == 'rs':
            d['sum'] = take()
        else:
            d['g'] = take()
            if ar['kind'] == 'attn':
                d['h'] = take()
    if kind == 'mlp':
        lhs, lhs_sem, gated, wbuf, w_sem = take(), take(), take(), take(), take()
    elif kind == 'head':
        lhs, x_sem, m_buf, w_a, w_b, w_sem, q_buf, k_buf, v_buf, o_buf = (take() for _ in range(10))
    if n_chunks:
        obuf, o_sem, os_sem, or_sem = take(), take(), take(), take()
    for d, ar in zip(ar_in, ars):
        for name in ar_scratch(ar['do']):
            d[name] = take()

    t = lax.axis_index('tp')
    core, xn, yn = {'tp': flip(t, 1)}, {'tp': flip(t, 2)}, {'tp': flip(t, 4)}
    step = pl.program_id(0)

    def rcopy(d, i, src, dst, dev):
        return Lazy(lambda: pltpu.make_async_remote_copy(src_ref=src, dst_ref=dst, send_sem=d['send'].at[i], recv_sem=d['recv'].at[i], device_id=dev, device_id_type=MESH))

    def lcopy(sem, src, dst):
        return Lazy(lambda: pltpu.make_async_copy(src, dst, sem))

    def at(ref, start, n):
        return ref.at[pl.ds(start, n)]

    def slots(d, first, n=1):
        return at(d['g'], first * piece, n * piece)

    def sum_loads(d, ar):
        out = []
        if ar['do'] == 'ag':
            return out
        for i, q in enumerate((1, 3, 0, 2)):
            for k, (src, dst) in enumerate(((d['own'], d['s']), (d['rcv'], d['r']))):
                out.append(lcopy(d['loc'].at[2 * i + k], at(src, q * quarter, quarter), at(dst, q * quarter, quarter)))
        return out

    def row_loads(d, ar):
        if ar['do'] == 'rs':
            return []
        if ar['kind'] == 'attn':
            res = at(d['res'], ar['chunk'] * rows + pl.multiple_of(t * quarter, quarter), quarter)
        else:
            res = d['res']
        out = [lcopy(d['loc'].at[8], res, d['x'])]
        if ar['do'] == 'ag':
            out.append(lcopy(d['loc'].at[0], d['sum'], d['n']))
        return out

    def sum_out(d):
        return lcopy(d['loc'].at[9], d['n'], d['sum'])

    def p1(d):
        def part(i, first, which, lo, dev):
            return rcopy(d, i, at(d['s'], first + lo, piece), d['r1'].at[which, pl.ds(lo, piece)], dev)
        return [part(0, quarter, 0, piece, xn), part(1, 3 * quarter, 1, piece, yn), part(16, quarter, 0, 0, xn), part(17, 3 * quarter, 1, 0, yn)]

    def p2(d):
        return [rcopy(d, 2, at(d['s'], piece, piece), d['r2'].at[0], yn), rcopy(d, 3, at(d['s'], 2 * quarter + piece, piece), d['r2'].at[1], xn)]

    def p3(d):
        a, b = at(d['n'], 0, piece), at(d['n'], piece, piece)
        return [rcopy(d, 4, a, slots(d, 1), yn), rcopy(d, 5, b, slots(d, 5), xn), rcopy(d, 6, a, slots(d, 2), xn), rcopy(d, 7, b, slots(d, 6), yn),
                rcopy(d, 10, a, slots(d, 8), core), rcopy(d, 11, b, slots(d, 12), core)]

    def own_out(d):
        return [lcopy(d['loc'].at[9], at(d['n'], 0, piece), slots(d, 0)), lcopy(d['loc'].at[10], at(d['n'], piece, piece), slots(d, 4))]

    def h_out(d):
        return lcopy(d['loc'].at[11], d['x'], d['h'])

    def p4(d):
        return [rcopy(d, 8, slots(d, 1), slots(d, 3), xn), rcopy(d, 9, slots(d, 5), slots(d, 7), yn)]

    def c1(d):
        return [rcopy(d, 12, slots(d, 1, 2), slots(d, 9, 2), core), rcopy(d, 13, slots(d, 5, 2), slots(d, 13, 2), core)]

    def c2(d):
        return [rcopy(d, 14, slots(d, 3), slots(d, 11), core), rcopy(d, 15, slots(d, 7), slots(d, 15), core)]

    def add_rows(dst, dst0, src, src0, n):
        def body(i, _):
            a = pl.ds(pl.multiple_of(dst0 + i * 16, 16), 16)
            b = pl.ds(pl.multiple_of(src0 + i * 16, 16), 16)
            dst[a, :] = (dst[a, :].astype(F32) + src[b, :].astype(F32)).astype(BF16)
            return 0
        lax.fori_loop(0, n // 16, body, 0)

    def ar_phase1(d, ar):
        loads, sends = sum_loads(d, ar), p1(d)
        for k, q in enumerate((1, 3)):
            loads[2 * k].wait()
            loads[2 * k + 1].wait()
            add_rows(d['s'], q * quarter + piece, d['r'], q * quarter + piece, piece)
            sends[k].start()
        for k, q in enumerate((1, 3)):
            add_rows(d['s'], q * quarter, d['r'], q * quarter, piece)
            sends[2 + k].start()
        for cp in loads[4:]:
            cp.wait()
        add_rows(d['s'], 0, d['r'], 0, quarter)
        add_rows(d['s'], 2 * quarter, d['r'], 2 * quarter, quarter)

    def ar_phase2(d, ar):
        for k in range(2):
            p1(d)[k].wait_recv()
            add_rows(d['s'], 2 * k * quarter + piece, d['r1'].at[k], piece, piece)
            p2(d)[k].start()

    def ar_finish(d, ar, part):
        base = part * piece
        src0 = part * 2 * quarter

        def body(i, _):
            here = pl.ds(pl.multiple_of(base + i * 16, 16), 16)
            there = pl.ds(pl.multiple_of(src0 + i * 16, 16), 16)
            other = pl.ds(pl.multiple_of(i * 16, 16), 16)
            if ar['do'] == 'ag':
                total = d['n'][here, :].astype(F32)
            else:
                total = d['s'][there, :].astype(F32) + d['r2'][part, other, :].astype(F32)
            if ar['do'] == 'rs':
                d['n'][here, :] = total.astype(BF16)
                return 0
            hid = (d['x'][here, :].astype(F32) + total).astype(BF16)
            if ar['kind'] == 'attn':
                d['x'][here, :] = hid
                hid = hid.astype(F32)
                mean_sq = jnp.sum(hid * hid, axis=-1, keepdims=True) / width
                hid = (hid * lax.rsqrt(mean_sq + EPSILON) * d['gain'][...].astype(F32)).astype(BF16)
            d['n'][here, :] = hid
            return 0
        lax.fori_loop(0, piece // 16, body, 0)

    def ar_phase3(d, ar):
        if ar['do'] != 'ag':
            for k in range(2):
                p1(d)[2 + k].wait_recv()
                add_rows(d['s'], 2 * k * quarter, d['r1'].at[k], 0, piece)
        for cp in row_loads(d, ar):
            cp.wait()
        for part in range(2):
            if ar['do'] != 'ag':
                p2(d)[part].wait_recv()
            ar_finish(d, ar, part)
            if ar['do'] != 'rs':
                p3(d)[part].start()
        if ar['do'] == 'rs':
            sum_out(d).start()
            return
        for cp in p3(d)[2:] + own_out(d):
            cp.start()
        if ar['kind'] == 'attn':
            h_out(d).start()

    def ar_phase4(d, ar):
        for k in range(2):
            p3(d)[k].wait_recv()
            p4(d)[k].start()

    def ar_phase5(d, ar):
        for k in range(2):
            p3(d)[2 + k].wait_recv()
            c1(d)[k].start()

    def ar_phase6(d, ar):
        for k in range(2):
            p4(d)[k].wait_recv()
            c2(d)[k].start()

    def ar_end(d, ar):
        if ar['do'] == 'rs':
            sum_out(d).wait()
        else:
            for cp in p3(d)[4:] + c1(d) + c2(d):
                cp.wait_recv()
            for cp in p3(d) + p4(d) + c1(d) + c2(d):
                cp.wait_send()
            for cp in own_out(d):
                cp.wait()
            if ar['kind'] == 'attn':
                h_out(d).wait()
        if ar['do'] != 'ag':
            for cp in p1(d) + p2(d):
                cp.wait_send()

    phase_sets = {'full': (ar_phase1, ar_phase2, ar_phase3, ar_phase4, ar_phase5, ar_phase6), 'rs': (ar_phase1, ar_phase2, ar_phase3),
                  'ag': (ar_phase3, ar_phase4, ar_phase5, ar_phase6)}

    def run_phases(k):
        for d, ar in zip(ar_in, ars):
            for when, phase in zip(ar['steps'], phase_sets[ar['do']]):
                if when == k:
                    phase(d, ar)

    def w_copies(j, n):
        slot = lax.rem(j, 2)
        cols = pl.ds(j * ffn_tile if isinstance(j, int) else pl.multiple_of(j * ffn_tile, ffn_tile), n)
        return [lcopy(w_sem.at[slot, 0], wg_hbm.at[:, cols], wbuf.at[slot, :, pl.ds(0, n)]),
                lcopy(w_sem.at[slot, 1], wu_hbm.at[:, cols], wbuf.at[slot, :, pl.ds(n, n)])]

    def lhs_copies():
        return [lcopy(lhs_sem.at[0], lhs_hbm, lhs)]

    def tile_copies(ci, j, slot):
        n = obuf.shape[2]
        cols = pl.ds(pl.multiple_of(j * n, n), n)
        return (lcopy(o_sem.at[slot], obuf.at[slot, pl.ds(0, half)], out_own[ci].at[:, cols]),
                Lazy(lambda: pltpu.make_async_remote_copy(src_ref=obuf.at[slot, pl.ds(half, half)], dst_ref=out_rcv[ci].at[:, cols],
                                             send_sem=os_sem.at[slot], recv_sem=or_sem.at[ci], device_id=core, device_id_type=MESH)))

    n_steps = cfg['n_steps']
    if kind == 'head':
        x_tile, heads, first = cfg['x_tile'], cfg['heads'], cfg['chunks'][0]
        tiles = rows // x_tile
        na = cfg['na']

    def x_copies(ci):
        return [lcopy(x_sem.at[i], at(x_hbm, pl.multiple_of((first + ci) * rows + i * x_tile, x_tile), x_tile), at(m_buf, i * x_tile, x_tile)) for i in range(tiles)]

    def qkv_copies():
        kv = pl.ds(pl.multiple_of(lax.div(t, cfg['kv_share']) * 128, 128), 128)
        cut, rest = na * 128, (heads - na) * 128
        return [lcopy(w_sem.at[0], wq_hbm.at[:, pl.ds(0, cut)], w_a), lcopy(w_sem.at[1], wq_hbm.at[:, pl.ds(cut, rest)], w_b.at[:, pl.ds(0, rest)]),
                lcopy(w_sem.at[2], wk_hbm.at[:, kv], w_b.at[:, pl.ds(rest, 128)]), lcopy(w_sem.at[3], wv_hbm.at[:, kv], w_b.at[:, pl.ds(rest + 128, 128)])]

    def norm_step(ci):
        cps = x_copies(ci)
        for tile in range(tiles):
            cps[tile].wait()

            def norm_rows(i, _):
                here = pl.ds(pl.multiple_of(tile * x_tile + i * 16, 16), 16)
                val = m_buf[here, :].astype(F32)
                mean_sq = jnp.sum(val * val, axis=-1, keepdims=True) / width
                m_buf[here, :] = (val * lax.rsqrt(mean_sq + EPSILON) * norm_ref[...].astype(F32)).astype(BF16)
                return 0
            lax.fori_loop(0, x_tile // 16, norm_rows, 0)

    def rotate(val, gain_ref):
        val = val * lax.rsqrt(jnp.sum(val * val, axis=-1, keepdims=True) / 128 + EPSILON) * gain_ref[...].astype(F32)
        return (val * cos_ref[...] + pltpu.roll(val, 64, 1) * sin_ref[...]).astype(BF16)

    def masked(ci, val):
        row = lax.broadcasted_iota(jnp.int32, (rows, 128), 0)
        return jnp.where(row < len_ref[first + ci], val.astype(F32), 0.0).astype(BF16)

    def query_step():
        proj = jnp.dot(m_buf[...], w_a[...], preferred_element_type=F32)
        for i in range(na):
            q_buf[i] = rotate(proj[:, i * 128:(i + 1) * 128], qg_ref)

    def last_step(ci):
        proj = jnp.dot(m_buf[...], w_b[...], preferred_element_type=F32)
        for i in range(na, heads):
            q_buf[i] = rotate(proj[:, (i - na) * 128:(i - na + 1) * 128], qg_ref)
        rest = (heads - na) * 128
        key = rotate(proj[:, rest:rest + 128], kg_ref)
        k_buf[...] = key
        kc_ref[...] = masked(ci, key)
        val = proj[:, rest + 128:].astype(BF16)
        v_buf[...] = val
        vc_ref[...] = masked(ci, val)

    def attention_step(ci, h):
        length = len_ref[first + ci]
        for i in range(tiles):
            n = (i + 1) * x_tile
            q = q_buf[h, i * x_tile:n, :]
            scores = lax.dot_general(q, k_buf[:n, :], (((1,), (1,)), ((), ())), preferred_element_type=F32) * 128 ** -0.5
            row = lax.broadcasted_iota(jnp.int32, (x_tile, n), 0) + i * x_tile
            col = lax.broadcasted_iota(jnp.int32, (x_tile, n), 1)
            scores = jnp.where((col <= row) & (col < length), scores, -1e30)
            weight = jnp.exp(scores - jnp.max(scores, axis=-1, keepdims=True))
            weight = (weight * (1.0 / jnp.sum(weight, axis=-1, keepdims=True))).astype(BF16)
            out = jnp.dot(weight, v_buf[:n, :], preferred_element_type=F32).astype(BF16)
            o_buf[i * x_tile:n, pl.ds(pl.multiple_of(h * 128, 128), 128)] = out

    def order_rows():
        for s in range(16):
            src = pl.ds(pl.multiple_of(origin_block(t, s) * piece, 16), piece)
            lhs[s * piece:(s + 1) * piece, :] = o_buf[src, :]

    @pl.when(step == 0)
    def _():
        for d, ar in zip(ar_in, ars):
            for cp in ([] if ar['source'] is not None else sum_loads(d, ar)) + row_loads(d, ar):
                cp.start()
        if kind == 'mlp':
            for cp in lhs_copies() + w_copies(0, ffn_tile):
                cp.start()
        if kind == 'head':
            for cp in x_copies(0) + qkv_copies():
                cp.start()
        barrier = pltpu.get_barrier_semaphore()
        for dev in (core, xn, yn):
            pl.semaphore_signal(barrier, inc=1, device_id=dev, device_id_type=MESH)
        pl.semaphore_wait(barrier, 3)
        run_phases(0)
        if kind == 'mlp':
            for cp in lhs_copies():
                cp.wait()

    for k in sorted({k for ar in ars for k in ar['steps']} - {0, END}):
        @pl.when(step == k)
        def _(k=k):
            run_phases(k)

    def drain(ci):
        for j in (cfg['per'] - 2, cfg['per'] - 1):
            a, b = tile_copies(ci, j, j % 2)
            a.wait()
            b.wait_send()
        pltpu.make_async_copy(out_rcv[ci], out_rcv[ci], or_sem.at[ci]).wait()

    def store_tile(ci, j, value):
        slot = lax.rem(j, 2)

        @pl.when(j >= 2)
        def _():
            a, b = tile_copies(ci, j, slot)
            a.wait()
            b.wait_send()
        obuf[slot] = value
        a, b = tile_copies(ci, j, slot)
        a.start()
        b.start()

    if kind == 'mlp':
        n_up = cfg['n_up']

        n_full, rest = cfg['n_full'], cfg['rest']

        @pl.when(step + 1 < n_full)
        def _():
            for cp in w_copies(step + 1, ffn_tile):
                cp.start()

        def gate_up(j, n):
            for cp in w_copies(j, n):
                cp.wait()
            both = jnp.dot(lhs[...], wbuf[lax.rem(j, 2), :, :2 * n], preferred_element_type=F32)
            gate = both[:, :n]
            gated[:, pl.ds(j * ffn_tile if isinstance(j, int) else pl.multiple_of(j * ffn_tile, ffn_tile), n)] = (gate * jax.nn.sigmoid(gate) * both[:, n:]).astype(BF16)

        if rest:
            @pl.when(step == n_full - 1)
            def _():
                for cp in w_copies(n_full, rest):
                    cp.start()

        @pl.when(step < n_full)
        def _():
            gate_up(step, ffn_tile)
        if rest:
            @pl.when(step == n_full)
            def _():
                gate_up(n_full, rest)

        @pl.when(step >= n_up)
        def _():
            store_tile(0, step - n_up, jnp.dot(gated[...], wd_ref[...], preferred_element_type=F32).astype(BF16))
    elif kind == 'head':
        per = cfg['per']
        ci = lax.div(step, cfg['chunk_steps'])
        sub = lax.rem(step, cfg['chunk_steps'])
        for c in range(n_chunks - 1):
            @pl.when(step == (c + 1) * cfg['chunk_steps'])
            def _(c=c):
                drain(c)
                for d, ar in zip(ar_in, ars):
                    if ar['source'] == c:
                        for cp in sum_loads(d, ar):
                            cp.start()

        begin = 2

        @pl.when(sub == 0)
        def _():
            norm_step(ci)
        for b, part in enumerate((slice(0, 1), slice(1, 4))):
            @pl.when(step == b)
            def _(part=part):
                for cp in qkv_copies()[part]:
                    cp.wait()
        pl.when(sub == 0)(query_step)

        @pl.when(sub == 1)
        def _():
            last_step(ci)

        @pl.when((sub == begin) & (ci + 1 < n_chunks))
        def _():
            for cp in x_copies(ci + 1):
                cp.start()

        @pl.when((sub >= begin) & (sub < begin + heads))
        def _():
            attention_step(ci, sub - begin)
        pl.when(sub == begin + heads)(order_rows)

        @pl.when(sub >= begin + heads)
        def _():
            value = jnp.dot(lhs[...], wo_ref[...], preferred_element_type=F32).astype(BF16)
            j = sub - begin - heads
            for c in range(n_chunks):
                @pl.when(ci == c)
                def _(c=c):
                    store_tile(c, j, value)

    @pl.when(step == n_steps - 1)
    def _():
        if n_chunks:
            drain(n_chunks - 1)
        for phase in (ar_phase1, ar_phase2, ar_phase3, ar_phase4, ar_phase5, ar_phase6):
            for d, ar in zip(ar_in, ars):
                for when, own_phase in zip(ar['steps'], phase_sets[ar['do']]):
                    if when == END and own_phase is phase:
                        phase(d, ar)
        for d, ar in zip(ar_in, ars):
            ar_end(d, ar)


def run_stage(cid, kind, compute, ars, rows, width, chunks=(), kv_share=1):
    any_spec = pl.BlockSpec(memory_space=pl.ANY)
    half, quarter, piece = rows // 2, rows // 8, rows // 16
    args, in_specs, out_shape, scratch = [], [], [], []
    out_tile = 512 if width % 512 == 0 else 128
    per = width // out_tile
    cfg = dict(kind=kind, width=width, rows=rows, chunks=chunks, per=per, ffn_tile=256,
               ars=[{k: a[k] for k in ('kind', 'chunk', 'do', 'steps', 'source')} for a in ars])
    if kind == 'mlp':
        n2, wg, wu, wd = compute
        ffn = wd.shape[0]
        n_full, rest = ffn // 256, ffn % 256
        n_up = n_full + (rest > 0)
        cfg.update(n_up=n_up, n_full=n_full, rest=rest, n_steps=n_up + per)
        args += [n2, wg, wu, wd]
        in_specs += [any_spec] * 3 + [pl.BlockSpec((ffn, out_tile), lambda j: (0, jnp.maximum(j - n_up, 0)))]
        scratch += [pltpu.VMEM((rows, width), BF16), pltpu.SemaphoreType.DMA((1,)), pltpu.VMEM((rows, ffn), BF16), pltpu.VMEM((2, width, 512), BF16), pltpu.SemaphoreType.DMA((2, 2))]
    elif kind == 'head':
        lengths, tokens, wq, wk, wv, norm, q_gain, k_gain, cosine, sine, wo = compute
        x_tile = rows // 3
        heads = wq.shape[1] // 128
        out_tile = 1024 if width % 1024 == 0 else out_tile
        per = width // out_tile
        begin = 2
        na = heads - 1
        chunk_steps = begin + heads + per
        first = chunks[0]
        cfg.update(n_steps=chunk_steps * len(chunks), x_tile=x_tile, heads=heads, chunk_steps=chunk_steps, kv_share=kv_share, per=per, na=na)
        args += [lengths, tokens, wq, wk, wv, norm, q_gain, k_gain, cosine, sine, wo]
        table = pl.BlockSpec((rows, 128), lambda j: (first + lax.div(j, chunk_steps), 0))
        gain_spec = pl.BlockSpec((1, 128), lambda j: (0, 0))
        in_specs += [pl.BlockSpec(memory_space=pltpu.SMEM)] + [any_spec] * 4 + [pl.BlockSpec((1, width), lambda j: (0, 0)), gain_spec, gain_spec, table, table,
                     pl.BlockSpec((heads * 128, out_tile), lambda j: (0, jnp.maximum(lax.rem(j, chunk_steps) - begin - heads, 0)))]
        scratch += [pltpu.VMEM((rows, heads * 128), BF16), pltpu.SemaphoreType.DMA((3,)), pltpu.VMEM((rows, width), BF16),
                    pltpu.VMEM((width, na * 128), BF16), pltpu.VMEM((width, (heads - na) * 128 + 256), BF16), pltpu.SemaphoreType.DMA((4,)),
                    pltpu.VMEM((heads, rows, 128), BF16), pltpu.VMEM((rows, 128), BF16), pltpu.VMEM((rows, 128), BF16), pltpu.VMEM((rows, heads * 128), BF16)]
        cache_spec = pl.BlockSpec((rows, 128), lambda j: (lax.div(j, chunk_steps), 0))
    else:
        cfg.update(n_steps=3)
    if chunks:
        scratch += [pltpu.VMEM((2, rows, out_tile), BF16), pltpu.SemaphoreType.DMA((2,)),
                    pltpu.SemaphoreType.DMA((2,)), pltpu.SemaphoreType.DMA((len(chunks),))]
    for a in ars:
        names = (() if a['do'] == 'ag' or a['source'] is not None else ('own', 'rcv')) + (('sum',) if a['do'] == 'ag' else ()) + (() if a['do'] == 'rs' else ('res',))
        args += [a[k] for k in names]
        in_specs += [any_spec] * len(names)
        if a['kind'] == 'attn' and a['do'] != 'rs':
            args.append(a['gain'])
            in_specs.append(pl.BlockSpec((1, width), lambda j: (0, 0)))
        sizes = dict(s=(half, width), r=(half, width), r1=(2, quarter, width), r2=(2, piece, width), x=(quarter, width), n=(quarter, width))
        counts = dict(send=18, recv=18, loc=12)
        scratch += [pltpu.VMEM(sizes[k], BF16) if k in sizes else pltpu.SemaphoreType.DMA((counts[k],)) for k in ar_scratch(a['do'])]
    for _ in chunks:
        out_shape += [jax.ShapeDtypeStruct((half, width), BF16)] * 2
    out_specs = [any_spec] * len(out_shape)
    if kind == 'head':
        out_shape += [jax.ShapeDtypeStruct((rows * len(chunks), 128), BF16)] * 2
        out_specs += [cache_spec] * 2
    for a in ars:
        if a['do'] == 'rs':
            out_shape.append(jax.ShapeDtypeStruct((quarter, width), BF16))
            continue
        out_shape.append(jax.ShapeDtypeStruct((rows, width), BF16))
        if a['kind'] == 'attn':
            out_shape.append(jax.ShapeDtypeStruct((quarter, width), BF16))
    return pl.pallas_call(
        functools.partial(stage_kernel, cfg),
        grid=(cfg['n_steps'],),
        out_shape=out_shape,
        in_specs=in_specs,
        out_specs=out_specs + [any_spec] * (len(out_shape) - len(out_specs)),
        scratch_shapes=scratch,
        compiler_params=pltpu.CompilerParams(collective_id=cid, has_side_effects=True, vmem_limit_bytes=62 * 1024 * 1024,
                                             dimension_semantics=('arbitrary',)),
        name=f'stage{cid}',
    )(*args)


def place_kernel(n, table_ref, *refs):
    for b in range(n):
        refs[n][b] = refs[b][...]


def place_rows(chunks, rows, width):
    t = lax.axis_index('tp')
    piece = rows // 16
    blocks = jnp.stack([jnp.asarray(origin_block(t, s), jnp.int32) for s in range(16)])
    table = jnp.argmax(blocks[None, :] == jnp.arange(16, dtype=jnp.int32)[:, None], axis=1).astype(jnp.int32)
    n = len(chunks)
    return pl.pallas_call(
        functools.partial(place_kernel, n),
        grid_spec=pltpu.PrefetchScalarGridSpec(
            num_scalar_prefetch=1, grid=(16,),
            in_specs=[pl.BlockSpec((piece, width), lambda k, tab: (tab[k], 0))] * n,
            out_specs=pl.BlockSpec((n, piece, width), lambda k, tab: (0, k, 0))),
        out_shape=jax.ShapeDtypeStruct((n, rows, width), BF16),
        name='place',
    )(table, *chunks)


def layer_body(tokens, positions, lengths, norm_attn, norm_mlp, q_gain, k_gain, w_query, w_key, w_value, w_out, w_gate, w_up, w_down, tp_size):
    num_prompts, seq_len, hidden_dim = tokens.shape
    head_dim = q_gain.shape[0]
    kv_heads = w_key.shape[1] // head_dim
    rows_n = num_prompts * seq_len
    tokens_flat = tokens.reshape(rows_n, hidden_dim)
    cosine, sine = rope_tables(positions, head_dim // 2)
    head_in = (lengths, tokens_flat, w_query, w_key, w_value, norm_attn.reshape(1, hidden_dim), q_gain.reshape(1, head_dim), k_gain.reshape(1, head_dim), cosine, sine, w_out)

    gain = norm_mlp.reshape(1, hidden_dim)
    stage = functools.partial(run_stage, rows=seq_len, width=hidden_dim, kv_share=tp_size // kv_heads)

    def attn_ar(do, chunk, steps, source=None, **arrays):
        return dict(kind='attn', do=do, chunk=chunk, steps=steps, source=source, res=tokens_flat, gain=gain, **arrays)

    def mlp_ar(steps, own, rcv, hid):
        return dict(kind='mlp', do='full', chunk=0, steps=steps, source=None, own=own, rcv=rcv, res=hid)

    weights = (w_gate, w_up, w_down)
    own0, rcv0, kc0, vc0 = stage(1, 'head', head_in, [], chunks=(0,))
    _, _, own2, rcv2, kc1, vc1, n0, h0, sum1 = stage(2, 'head', head_in, [
        attn_ar('full', 0, (0, 1, 11, 13, 15, 18), own=own0, rcv=rcv0), attn_ar('rs', 1, (13, 19, END), source=0)], chunks=(1, 2))
    m_own0, m_rcv0, sum2, n1, h1 = stage(3, 'mlp', (n0, *weights), [
        attn_ar('rs', 2, (0, 2, END), own=own2, rcv=rcv2), attn_ar('ag', 1, (0, 6, END, END), sum=sum1)], chunks=(0,))
    m_own1, m_rcv1, out0, n2, h2 = stage(4, 'mlp', (n1, *weights), [
        mlp_ar((0, 2, 10, END, END, END), m_own0, m_rcv0, h0), attn_ar('ag', 2, (0, 6, END, END), sum=sum2)], chunks=(1,))
    m_own2, m_rcv2, out1 = stage(5, 'mlp', (n2, *weights), [mlp_ar((0, 2, 7, 11, END, END), m_own1, m_rcv1, h1)], chunks=(2,))
    out2, = stage(6, 'none', (), [mlp_ar((0, 0, 1, 2, END, END), m_own2, m_rcv2, h2)])
    k_parts, v_parts = [kc0, kc1], [vc0, vc1]
    cache_shape = (num_prompts, seq_len, 1, head_dim)
    k_cache = jnp.concatenate(k_parts).reshape(cache_shape)
    v_cache = jnp.concatenate(v_parts).reshape(cache_shape)
    output = place_rows([out0, out1, out2], seq_len, hidden_dim)
    return output, k_cache, v_cache


def solution(mesh):
    body = functools.partial(layer_body, tp_size=mesh.shape['tp'])
    in_specs = (P('dp', None, None), P('dp', None), P('dp'), P(), P(), P(), P(), P(None, 'tp'), P(), P(), P('tp', None), P(None, 'tp'), P(None, 'tp'), P('tp', None))
    out_specs = (P('dp', None, None), P('dp', None, 'tp', None), P('dp', None, 'tp', None))
    return jax.shard_map(body, mesh=mesh, in_specs=in_specs, out_specs=out_specs, check_vma=False)
```

time: 645 us -> 538 us (0.83)
  matrix products: 77.1 us -> 0 us
  other arithmetic: 30.5 us -> 11.3 us
  local copies, waits for them, and re-layouts: 19.7 us -> 2.74 us
  Pallas kernels: 506 us -> 517 us
    dot_general x4 -> x0, matrix products: 58.2 us -> none  [the longest x1 21.8 us: layer_body(): jnp.dot(normed, w_query, preferred_element_type=F32)]
    sub x1 -> x0, matrix products: 18.9 us -> none  [local_attention(): jax.nn.softmax(jnp.where(allowed, scores, -1e+30), axis=-1).astype(BF16)]
    unnamed x16 -> x4, local copies, waits for them, and re-layouts: 14.4 us -> 0.01 us
    pallas_call x6, Pallas kernels: 484 us -> 495 us  [run_stage(): pl.pallas_call(functools.partial(stage_kernel, cfg), grid=(cfg['n_steps']...]
    reduce_sum x1 -> x0, other arithmetic: 9.97 us -> none  [rms_scale(): mean_sq = jnp.mean(values * values, axis=-1, keepdims=True)]
    another operation x2 -> x0, other arithmetic: 8.56 us -> none
where the time goes in v2:
time: 538 us; the launch traced here: 532 us
  Pallas kernels  517 us (96%)
  other arithmetic  11.3 us (2%)
    pallas_call x6, Pallas kernels, run_stage(): pl.pallas_call(functools.partial(stage_kernel, cfg), grid=(cfg['n_steps']...  495 us
    pallas_call x1, Pallas kernels, place_rows(): pl.pallas_call(functools.partial(place_kernel, n), grid_spec=pltpu.Prefet...  21.7 us

profile of v2, /device:TPU:0, one launch (start us, length us, event | category | flops | bytes accessed | tf_op | source)
XLA Modules:
  0.0 532.3 jit_solution(6656182920829357179)
XLA Ops:
  0.7 0.1 stack.67
  0.8 0.6 iota_reduce_fusion
  1.5 0.7 convert_element_type.3
  2.2 1.3 reshape.40.refs_14_.refs_8_.refs_9_
  3.5 1.3 reshape.37.refs_5_
  4.8 4.2 fusion
  9.0 2.1 pad_maximum_fusion
  11.1 45.7 %stage1.1 = (bf16[384,5120]{1,0:T(8,128)(2,1)}, bf16[384,5120]{1,0:T(8,128)(2,1)}, bf16[768,128]{1,0:T(8,128)(2,1)}, bf16[768,128]{1,0:T(8,128)(2,1)}) custom-call(s32[3]{0:T(128)} %refs_0_.3, bf16[2304,5120]{1,0:T(8,128)(2,1)} %bitcast.25, bf16[5120,640]{1,0:T(8,128)(2,1)} %refs_2_.6, bf16[5120,1024]{1,0:T(8,128)(2,1)} %refs_3_.6, ...), custom_call_target="tpu_custom_call" | custom-call | tf_op jit(solution)/shard_map/stage1/pallas_call | solution.py:586
  56.8 0.0 copy-start.1
  56.8 0.0 copy-start
  56.8 115.9 %stage2.1 = (bf16[384,5120]{1,0:T(8,128)(2,1)}, bf16[384,5120]{1,0:T(8,128)(2,1)}, bf16[384,5120]{1,0:T(8,128)(2,1)}, bf16[384,5120]{1,0:T(8,128)(2,1)}, bf16[15...) custom-call(s32[3]{0:T(128)} %refs_0_.3, ...), custom_call_target="tpu_custom_call" | custom-call | tf_op jit(solution)/shard_map/stage2/pallas_call | solution.py:586
  172.7 0.0 copy-done.1
  172.7 1.9 pad_maximum_fusion.2
  174.6 0.0 copy-done
  174.6 1.8 pad_maximum_fusion.3
  176.4 79.0 %stage3.1 = (bf16[384,5120]{1,0:T(8,128)(2,1)}, bf16[384,5120]{1,0:T(8,128)(2,1)}, bf16[96,5120]{1,0:T(8,128)(2,1)}, bf16[768,5120]{1,0:T(8,128)(2,1)}, bf16[96,5120]{1,0:T(8,128)(2,1)}) custom-call(bf16[768,5120]{1,0:T(8,128)(2,1)} %get-tuple-element.31.refs_0_, bf16[5120,2176]{1,0:T(8,128)(2,1)} %refs_1_.5, bf16[5120,2176]{1,0:T(8,128)(2,1)} %refs_2_.9, ...), custom_call_target="tpu_custom_call" | custom-call | tf_op jit(solution)/shard_map/stage3/pallas_call | solution.py:586
  255.4 104.2 %stage4.1 = (bf16[384,5120]{1,0:T(8,128)(2,1)}, bf16[384,5120]{1,0:T(8,128)(2,1)}, bf16[768,5120]{1,0:T(8,128)(2,1)}, bf16[768,5120]{1,0:T(8,128)(2,1)}, bf16[96,5120]{1,0:T(8,128)(2,1)}) custom-call(bf16[768,5120]{1,0:T(8,128)(2,1)} %get-tuple-element.35.refs_0_, bf16[5120,2176]{1,0:T(8,128)(2,1)} %refs_1_.5, bf16[5120,2176]{1,0:T(8,128)(2,1)} %refs_2_.9, ...), custom_call_target="tpu_custom_call" | custom-call | tf_op jit(solution)/shard_map/stage4/pallas_call | solution.py:586
  359.6 78.8 %stage5.1 = (bf16[384,5120]{1,0:T(8,128)(2,1)}, bf16[384,5120]{1,0:T(8,128)(2,1)}, bf16[768,5120]{1,0:T(8,128)(2,1)}) custom-call(bf16[768,5120]{1,0:T(8,128)(2,1)} %get-tuple-element.41.refs_0_, bf16[5120,2176]{1,0:T(8,128)(2,1)} %refs_1_.5, bf16[5120,2176]{1,0:T(8,128)(2,1)} %refs_2_.9, bf16[2176,5120]{1,0:T(8,128)(2,1)} %refs_3_.9, ...), custom_call_target="tpu_custom_call" | custom-call | tf_op jit(solution)/shard_map/stage5/pallas_call | solution.py:586
  438.4 71.9 %stage6.1.refs_2_ = bf16[768,5120]{1,0:T(8,128)(2,1)} custom-call(bf16[384,5120]{1,0:T(8,128)(2,1)} %get-tuple-element.46.refs_0_, bf16[384,5120]{1,0:T(8,128)(2,1)} %get-tuple-element.47.refs_1_, bf16[96,5120]{1,0:T(8,128)(2,1)} %get-tuple-element.48.refs_2_), custom_call_target="tpu_custom_call" | custom-call | tf_op jit(solution)/shard_map/stage6/pallas_call | solution.py:586
  510.3 21.7 %place.1 = bf16[3,768,5120]{2,1,0:T(8,128)(2,1)} custom-call(s32[16]{0:T(128)} %get-tuple-element.28.table_ref, bf16[768,5120]{1,0:T(8,128)(2,1)} %get-tuple-element.40.refs_0_, bf16[768,5120]{1,0:T(8,128)(2,1)} %get-tuple-element.45.refs_1_, bf16[768,5120]{1,0:T(8,128)(2,1)} %stage6.1.refs_2_), custom_call_target="tpu_custom_call" | custom-call | tf_op jit(solution)/shard_map/place/pallas_call | solution.py:610
  (2 shorter events, 0.0 us)
Async XLA Ops:
  56.8 115.9 %copy-start.1 = (bf16[768,128]{1,0:T(8,128)(2,1)S(1)}, bf16[768,128]{1,0:T(8,128)(2,1)}, u32[]{:S(2)}) copy-start(bf16[768,128]{1,0:T(8,128)(2,1)} %get-tuple-element.49) | copy-start | bytes 589828
  56.8 117.8 %copy-start = (bf16[768,128]{1,0:T(8,128)(2,1)S(1)}, bf16[768,128]{1,0:T(8,128)(2,1)}, u32[]{:S(2)}) copy-start(bf16[768,128]{1,0:T(8,128)(2,1)} %get-tuple-element.51) | copy-start | bytes 589828

commit v3 on v2

--- a/solution.py
+++ b/solution.py
@@ -176,12 +176,16 @@
         return [rcopy(d, 14, slots(d, 3), slots(d, 11), core), rcopy(d, 15, slots(d, 7), slots(d, 15), core)]
 
     def add_rows(dst, dst0, src, src0, n):
+        cols_n = width // 4 if width % 512 == 0 else width
+
         def body(i, _):
-            a = pl.ds(pl.multiple_of(dst0 + i * 16, 16), 16)
-            b = pl.ds(pl.multiple_of(src0 + i * 16, 16), 16)
-            dst[a, :] = (dst[a, :].astype(F32) + src[b, :].astype(F32)).astype(BF16)
+            row, col = lax.div(i, width // cols_n) * 16, lax.rem(i, width // cols_n) * cols_n
+            a = pl.ds(pl.multiple_of(dst0 + row, 16), 16)
+            b = pl.ds(pl.multiple_of(src0 + row, 16), 16)
+            c = pl.ds(pl.multiple_of(col, 128), cols_n)
+            dst[a, c] = (dst[a, c].astype(F32) + src[b, c].astype(F32)).astype(BF16)
             return 0
-        lax.fori_loop(0, n // 16, body, 0)
+        lax.fori_loop(0, n // 16 * (width // cols_n), body, 0)
 
     def ar_phase1(d, ar):
         loads, sends = sum_loads(d, ar), p1(d)
@@ -322,17 +326,20 @@
                 lcopy(w_sem.at[2], wk_hbm.at[:, kv], w_b.at[:, pl.ds(rest, 128)]), lcopy(w_sem.at[3], wv_hbm.at[:, kv], w_b.at[:, pl.ds(rest + 128, 128)])]
 
     def norm_step(ci):
-        cps = x_copies(ci)
-        for tile in range(tiles):
-            cps[tile].wait()
-
-            def norm_rows(i, _):
-                here = pl.ds(pl.multiple_of(tile * x_tile + i * 16, 16), 16)
-                val = m_buf[here, :].astype(F32)
-                mean_sq = jnp.sum(val * val, axis=-1, keepdims=True) / width
-                m_buf[here, :] = (val * lax.rsqrt(mean_sq + EPSILON) * norm_ref[...].astype(F32)).astype(BF16)
-                return 0
-            lax.fori_loop(0, x_tile // 16, norm_rows, 0)
+        per_tile = x_tile // 16
+
+        def norm_rows(i, _):
+            @pl.when(lax.rem(i, per_tile) == 0)
+            def _():
+                tile = lax.div(i, per_tile)
+                dst = at(m_buf, pl.multiple_of(tile * x_tile, x_tile), x_tile)
+                lcopy(x_sem.at[tile], at(x_hbm, pl.multiple_of((first + ci) * rows + tile * x_tile, x_tile), x_tile), dst).wait()
+            here = pl.ds(pl.multiple_of(i * 16, 16), 16)
+            val = m_buf[here, :].astype(F32)
+            mean_sq = jnp.sum(val * val, axis=-1, keepdims=True) / width
+            m_buf[here, :] = (val * lax.rsqrt(mean_sq + EPSILON) * norm_ref[...].astype(F32)).astype(BF16)
+            return 0
+        lax.fori_loop(0, rows // 16, norm_rows, 0)
 
     def rotate(val, gain_ref):
         val = val * lax.rsqrt(jnp.sum(val * val, axis=-1, keepdims=True) / 128 + EPSILON) * gain_ref[...].astype(F32)
@@ -639,7 +646,7 @@
     weights = (w_gate, w_up, w_down)
     own0, rcv0, kc0, vc0 = stage(1, 'head', head_in, [], chunks=(0,))
     _, _, own2, rcv2, kc1, vc1, n0, h0, sum1 = stage(2, 'head', head_in, [
-        attn_ar('full', 0, (0, 1, 11, 13, 15, 18), own=own0, rcv=rcv0), attn_ar('rs', 1, (13, 19, END), source=0)], chunks=(1, 2))
+        attn_ar('full', 0, (0, 1, 9, 13, 15, 18), own=own0, rcv=rcv0), attn_ar('rs', 1, (13, 19, END), source=0)], chunks=(1, 2))
     m_own0, m_rcv0, sum2, n1, h1 = stage(3, 'mlp', (n0, *weights), [
         attn_ar('rs', 2, (0, 2, END), own=own2, rcv=rcv2), attn_ar('ag', 1, (0, 6, END, END), sum=sum1)], chunks=(0,))
     m_own1, m_rcv1, out0, n2, h2 = stage(4, 'mlp', (n1, *weights), [

time: 538 us -> 537 us (level)
  no operation moved by 1% of the time
where the time goes in v3:
time: 537 us; the launch traced here: 532 us
  Pallas kernels  517 us (96%)
  other arithmetic  11.3 us (2%)
    pallas_call x6, Pallas kernels, run_stage(): pl.pallas_call(functools.partial(stage_kernel, cfg), grid=(cfg['n_steps']...  495 us
    pallas_call x1, Pallas kernels, place_rows(): pl.pallas_call(functools.partial(place_kernel, n), grid_spec=pltpu.Prefet...  21.7 us

profile of v3, /device:TPU:0, one launch (start us, length us, event | category | flops | bytes accessed | tf_op | source)
XLA Modules:
  0.0 531.9 jit_solution(2922889055424383876)
XLA Ops:
  0.7 0.1 stack.67
  0.8 0.6 iota_reduce_fusion
  1.5 0.7 convert_element_type.3
  2.2 1.3 reshape.40.refs_14_.refs_8_.refs_9_
  3.5 1.3 reshape.37.refs_5_
  4.8 4.2 fusion
  9.0 2.1 pad_maximum_fusion
  11.1 45.6 %stage1.1 = (bf16[384,5120]{1,0:T(8,128)(2,1)}, bf16[384,5120]{1,0:T(8,128)(2,1)}, bf16[768,128]{1,0:T(8,128)(2,1)}, bf16[768,128]{1,0:T(8,128)(2,1)}) custom-call(s32[3]{0:T(128)} %refs_0_.3, bf16[2304,5120]{1,0:T(8,128)(2,1)} %bitcast.25, bf16[5120,640]{1,0:T(8,128)(2,1)} %refs_2_.6, bf16[5120,1024]{1,0:T(8,128)(2,1)} %refs_3_.6, ...), custom_call_target="tpu_custom_call" | custom-call | tf_op jit(solution)/shard_map/stage1/pallas_call | solution.py:593
  56.7 0.0 copy-start.1
  56.7 0.0 copy-start
  56.7 114.7 %stage2.1 = (bf16[384,5120]{1,0:T(8,128)(2,1)}, bf16[384,5120]{1,0:T(8,128)(2,1)}, bf16[384,5120]{1,0:T(8,128)(2,1)}, bf16[384,5120]{1,0:T(8,128)(2,1)}, bf16[15...) custom-call(s32[3]{0:T(128)} %refs_0_.3, ...), custom_call_target="tpu_custom_call" | custom-call | tf_op jit(solution)/shard_map/stage2/pallas_call | solution.py:593
  171.4 0.0 copy-done.1
  171.4 1.9 pad_maximum_fusion.2
  173.3 0.0 copy-done
  173.3 1.8 pad_maximum_fusion.3
  175.1 79.1 %stage3.1 = (bf16[384,5120]{1,0:T(8,128)(2,1)}, bf16[384,5120]{1,0:T(8,128)(2,1)}, bf16[96,5120]{1,0:T(8,128)(2,1)}, bf16[768,5120]{1,0:T(8,128)(2,1)}, bf16[96,5120]{1,0:T(8,128)(2,1)}) custom-call(bf16[768,5120]{1,0:T(8,128)(2,1)} %get-tuple-element.31.refs_0_, bf16[5120,2176]{1,0:T(8,128)(2,1)} %refs_1_.5, bf16[5120,2176]{1,0:T(8,128)(2,1)} %refs_2_.9, ...), custom_call_target="tpu_custom_call" | custom-call | tf_op jit(solution)/shard_map/stage3/pallas_call | solution.py:593
  254.2 104.4 %stage4.1 = (bf16[384,5120]{1,0:T(8,128)(2,1)}, bf16[384,5120]{1,0:T(8,128)(2,1)}, bf16[768,5120]{1,0:T(8,128)(2,1)}, bf16[768,5120]{1,0:T(8,128)(2,1)}, bf16[96,5120]{1,0:T(8,128)(2,1)}) custom-call(bf16[768,5120]{1,0:T(8,128)(2,1)} %get-tuple-element.35.refs_0_, bf16[5120,2176]{1,0:T(8,128)(2,1)} %refs_1_.5, bf16[5120,2176]{1,0:T(8,128)(2,1)} %refs_2_.9, ...), custom_call_target="tpu_custom_call" | custom-call | tf_op jit(solution)/shard_map/stage4/pallas_call | solution.py:593
  358.7 79.0 %stage5.1 = (bf16[384,5120]{1,0:T(8,128)(2,1)}, bf16[384,5120]{1,0:T(8,128)(2,1)}, bf16[768,5120]{1,0:T(8,128)(2,1)}) custom-call(bf16[768,5120]{1,0:T(8,128)(2,1)} %get-tuple-element.41.refs_0_, bf16[5120,2176]{1,0:T(8,128)(2,1)} %refs_1_.5, bf16[5120,2176]{1,0:T(8,128)(2,1)} %refs_2_.9, bf16[2176,5120]{1,0:T(8,128)(2,1)} %refs_3_.9, ...), custom_call_target="tpu_custom_call" | custom-call | tf_op jit(solution)/shard_map/stage5/pallas_call | solution.py:593
  437.7 72.2 %stage6.1.refs_2_ = bf16[768,5120]{1,0:T(8,128)(2,1)} custom-call(bf16[384,5120]{1,0:T(8,128)(2,1)} %get-tuple-element.46.refs_0_, bf16[384,5120]{1,0:T(8,128)(2,1)} %get-tuple-element.47.refs_1_, bf16[96,5120]{1,0:T(8,128)(2,1)} %get-tuple-element.48.refs_2_), custom_call_target="tpu_custom_call" | custom-call | tf_op jit(solution)/shard_map/stage6/pallas_call | solution.py:593
  509.9 21.7 %place.1 = bf16[3,768,5120]{2,1,0:T(8,128)(2,1)} custom-call(s32[16]{0:T(128)} %get-tuple-element.28.table_ref, bf16[768,5120]{1,0:T(8,128)(2,1)} %get-tuple-element.40.refs_0_, bf16[768,5120]{1,0:T(8,128)(2,1)} %get-tuple-element.45.refs_1_, bf16[768,5120]{1,0:T(8,128)(2,1)} %stage6.1.refs_2_), custom_call_target="tpu_custom_call" | custom-call | tf_op jit(solution)/shard_map/place/pallas_call | solution.py:617
  (2 shorter events, 0.0 us)
Async XLA Ops:
  56.7 114.8 %copy-start.1 = (bf16[768,128]{1,0:T(8,128)(2,1)S(1)}, bf16[768,128]{1,0:T(8,128)(2,1)}, u32[]{:S(2)}) copy-start(bf16[768,128]{1,0:T(8,128)(2,1)} %get-tuple-element.49) | copy-start | bytes 589828
  56.7 116.6 %copy-start = (bf16[768,128]{1,0:T(8,128)(2,1)S(1)}, bf16[768,128]{1,0:T(8,128)(2,1)}, u32[]{:S(2)}) copy-start(bf16[768,128]{1,0:T(8,128)(2,1)} %get-tuple-element.51) | copy-start | bytes 589828
